TPU v7x, 512 devices: a whole 4x8x8 slice. The times are simulated.
512 devices in a mesh: batch: 128 (over x, y_lo, z), mp: 4 (over y_hi, core).
Axes of the slice: x: 4, y: 8 (y_hi: 2, y_lo: 4; y = y_hi * 4 + y_lo), z: 8, core: 2. Of those that a mesh axis runs over, the one named last changes fastest.
Arguments:
- img_feat: bfloat16 [2048, 1536], P('batch'), may hold values from -6 to 6
- txt_feat: bfloat16 [2048, 1536], P('batch'), may hold values from -6 to 6
- w_img: bfloat16 [1536, 1152], P('batch', 'mp'), may hold values from -0.15625 to 0.15625
- w_txt: bfloat16 [1536, 1152], P('batch', 'mp'), may hold values from -0.15625 to 0.15625
- pair_index: int32 [2048], P('batch'), may hold values from 0 to 2047, each once
- log_scale: float32 [1], replicated, may hold values from 2 to 2.6
- bias: float32 [1], replicated, may hold values from -6 to -4
Outputs:
- image_grad: float32 [2048, 1152], P('batch', 'mp')
- text_grad: float32 [2048, 1152], P(('batch', 'mp'))
Inputs may be any that keep to these rules, and one draw needn't show every extreme that they name: `pair_index`: each text index appears exactly once.
All inputs are finite; a program needn't handle non-finite values.
Results may differ from a plain program's by a relative error of at most 0.0046.
Values may be sent and summed in bfloat16 or wider, within the bound.
No kernel may reach another device: no remote copies, remote signals or barrier semaphores. Data moves between devices by JAX's collectives and lax.ppermute only.
A program may use at most 64 MiB of HBM per device.

v0:
```python
import jax
import jax.numpy as jnp
from jax import lax
from jax.sharding import Mesh
from jax.sharding import PartitionSpec as P

BATCH = ("batch_0", "batch_1", "batch_2")
MP = ("mp_0", "mp_1")
BATCH_MP = ("batch_0", "batch_1", "batch_2", "mp_0", "mp_1")
epsilon = 1e-06


def joined_along(pieces, dim):
    lengths = list(pieces.shape[1:])
    lengths[dim] *= pieces.shape[0]
    return jnp.moveaxis(pieces, 0, dim).reshape(lengths)


def stacked_from(x, axes, order):
    pieces = x[None]
    for k in order:
        pieces = lax.all_gather(pieces, axes[k], axis=0, tiled=True)
    current = [lax.axis_size(axes[k]) for k in reversed(order)]
    pieces = pieces.reshape(*current, *x.shape)
    turned = sorted(range(len(order)), key=lambda place: order[len(order) - 1 - place])
    return pieces.transpose(*turned, *range(len(order), pieces.ndim)).reshape(-1, *x.shape)


def gathered_by_axis(x, axes, order, dim):
    return joined_along(stacked_from(x, axes, order), dim)


def from_behind(value, axis, steps):
    count = lax.axis_size(axis)
    pairs = [(source, (source + steps) % count) for source in range(count)]
    return lax.ppermute(value, axis, pairs)


def in_blocks(x, dim, size):
    before, after = (x.shape[:dim], x.shape[dim + 1 :])
    return jnp.moveaxis(x.reshape(*before, size, -1, *after), dim, 0)


def sent_and_summed(x, axis, dim):
    pieces = in_blocks(x, dim, lax.axis_size(axis))
    arrived = lax.all_to_all(pieces, axis, split_axis=0, concat_axis=0, tiled=True)
    return arrived.sum(axis=0)


def normalize(pre):
    values = pre.astype(jnp.float32)
    norm = lax.rsqrt(jnp.sum(values * values, axis=1, keepdims=True) + epsilon)
    return (values * norm).astype(jnp.bfloat16)


def block_update(image, pairing, scale, offset, text, first):
    count = text.shape[0]
    scores = lax.dot_general(
        image, text, (((1,), (1,)), ((), ())), preferred_element_type=jnp.float32
    )
    logits = scale * scores + offset
    columns = first + jnp.arange(count, dtype=jnp.int32)
    label = jnp.where(pairing[:, None] == columns[None, :], 1.0, -1.0).astype(jnp.float32)
    coef = (-label * jax.nn.sigmoid(-label * logits)).astype(jnp.bfloat16)
    image_term = jnp.dot(coef, text, preferred_element_type=jnp.float32)
    text_term = lax.dot_general(
        coef, image, (((0,), (0,)), ((), ())), preferred_element_type=jnp.float32
    )
    return (image_term, text_term)


def local(img_feat, txt_feat, w_img, w_txt, pair_index, log_scale, bias):
    rows = img_feat.shape[0]
    cycle_size = lax.axis_size(BATCH)
    group_size = lax.axis_size(MP)
    here = lax.axis_index(BATCH)
    member = lax.axis_index(MP)
    piece_rows = rows // group_size
    columns_part = w_img.shape[1]
    width = group_size * columns_part
    span = min(cycle_size, 32)
    half = span // 2
    first = jnp.dot(
        img_feat, gathered_by_axis(w_img, BATCH, (1, 2, 0), 0), preferred_element_type=jnp.float32
    )
    second = jnp.dot(
        txt_feat, gathered_by_axis(w_txt, BATCH, (1, 2, 0), 0), preferred_element_type=jnp.float32
    )
    full_img, full_txt = (
        gathered_by_axis(first.astype(jnp.bfloat16), MP, (0, 1), 1),
        gathered_by_axis(second.astype(jnp.bfloat16), MP, (0, 1), 1),
    )
    image = normalize(full_img)
    own_start = member * piece_rows
    text = normalize(lax.dynamic_slice_in_dim(full_txt, own_start, piece_rows, 0))
    scale = jnp.exp(log_scale[0])
    offset = bias[0]
    image_total = jnp.zeros((rows, width), jnp.float32)
    start_grads = jnp.zeros((piece_rows, width), jnp.float32)

    def first_row(anchor):
        return anchor * rows + member * piece_rows

    def turn_front(step, carry):
        front, front_acc, totals = carry
        anchor = (here - step) % cycle_size
        image_term, text_term = block_update(
            image, pair_index, scale, offset, front, first_row(anchor)
        )
        front = from_behind(front, BATCH, 1)
        front_acc = from_behind(front_acc + text_term, BATCH, 1)
        return (front, front_acc, totals + image_term)

    def turn_rear(step, carry):
        rear, rear_acc, totals = carry
        rear = from_behind(rear, BATCH, -1)
        rear_acc = from_behind(rear_acc, BATCH, -1)
        anchor = (here + step + 1) % cycle_size
        image_term, text_term = block_update(
            image, pair_index, scale, offset, rear, first_row(anchor)
        )
        return (rear, rear_acc + text_term, totals + image_term)

    front, front_acc, image_total = lax.fori_loop(
        0, half, turn_front, (text, start_grads, image_total)
    )
    rear, rear_acc, image_total = lax.fori_loop(
        0, half, turn_rear, (text, start_grads, image_total)
    )
    front_back = from_behind(front_acc, BATCH, -half)
    rear_back = from_behind(rear_acc, BATCH, half)
    text_total = front_back + rear_back
    image_part = sent_and_summed(image_total, MP, 1)
    return (scale * image_part, scale * text_total)


def solution(mesh):
    finer = Mesh(
        mesh.devices.reshape(4, 4, 8, 2, 2), ("batch_0", "batch_1", "batch_2", "mp_0", "mp_1")
    )
    in_specs = (P(BATCH, None), P(BATCH, None), P(BATCH, MP), P(BATCH, MP), P(BATCH), P(), P())
    out_specs = (P(BATCH, MP), P(BATCH_MP, None))
    return jax.shard_map(local, mesh=finer, in_specs=in_specs, out_specs=out_specs, check_vma=False)
```

profile of v0, /device:TPU:1, one launch (start us, length us, event | category | flops | bytes accessed | tf_op | source)
XLA Modules:
  0.0 614.7 jit_solution(6283159459050296204)
XLA Ops:
  0.7 11.5 %all-gather.4 = bf16[4,12,288]{2,1,0:T(8,128)(2,1)S(1)} all-gather(bf16[1,12,288]{2,1,0:T(8,128)(2,1)} %bitcast.76), channel_id=2, replica_groups=mesh['batch_0'=4,'batch_1'=4,'batch_2'=8,'mp_0'=2,'mp_1'=2] {'batch_1'}, dimensions={0}, use_global_device_ids=true | all-gather | bytes 34560 | tf_op jit(solution)/shard_map/all_gather | solution.py:22
  12.1 26.0 %all_gather.31 = bf16[32,12,288]{2,1,0:T(8,128)(2,1)S(1)} all-gather(bf16[4,12,288]{2,1,0:T(8,128)(2,1)S(1)} %all-gather.4), channel_id=1, replica_groups=mesh['batch_0'=4,'batch_1'=4,'batch_2'=8,'mp_0'=2,'mp_1'=2] {'batch_2'}, dimensions={0}, use_global_device_ids=true | all-gather | bytes 248832 | tf_op jit(solution)/shard_map/all_gather | solution.py:22
  38.2 12.2 %all_gather.32 = bf16[128,12,288]{2,0,1:T(8,128)(2,1)S(1)} all-gather(bf16[32,12,288]{2,0,1:T(8,128)(2,1)S(1)} %copy.24), channel_id=1, replica_groups=mesh['batch_0'=4,'batch_1'=4,'batch_2'=8,'mp_0'=2,'mp_1'=2] {'batch_0'}, dimensions={0}, use_global_device_ids=true | all-gather | bytes 1105920 | tf_op jit(solution)/shard_map/all_gather | solution.py:22
  52.4 7.2 %all-gather.1 = bf16[32,288]{1,0:T(8,128)(2,1)S(1)} all-gather(bf16[16,288]{1,0:T(8,128)(2,1)S(1)} %convolution_convert_fusion.1), channel_id=3, replica_groups=mesh['batch_0'=4,'batch_1'=4,'batch_2'=8,'mp_0'=2,'mp_1'=2] {'mp_0'}, dimensions={0}, use_global_device_ids=true | all-gather | bytes 27648 | tf_op jit(solution)/shard_map/all_gather | solution.py:22
  59.6 14.0 %all_gather.34 = bf16[4,16,288]{2,1,0:T(8,128)(2,1)S(1)} all-gather(bf16[2,16,288]{2,1,0:T(8,128)(2,1)S(1)} %bitcast.74), channel_id=1, replica_groups=mesh['batch_0'=4,'batch_1'=4,'batch_2'=8,'mp_0'=2,'mp_1'=2] {'mp_1'}, dimensions={0}, use_global_device_ids=true | all-gather | bytes 55296 | tf_op jit(solution)/shard_map/all_gather | solution.py:22
  73.9 10.2 %all-gather.5 = bf16[4,12,288]{2,1,0:T(8,128)(2,1)S(1)} all-gather(bf16[1,12,288]{2,1,0:T(8,128)(2,1)S(1)} %bitcast.77), channel_id=4, replica_groups=mesh['batch_0'=4,'batch_1'=4,'batch_2'=8,'mp_0'=2,'mp_1'=2] {'batch_1'}, dimensions={0}, use_global_device_ids=true | all-gather | bytes 34560 | tf_op jit(solution)/shard_map/all_gather | solution.py:22
  84.2 19.4 %all_gather.36 = bf16[32,12,288]{2,1,0:T(8,128)(2,1)S(1)} all-gather(bf16[4,12,288]{2,1,0:T(8,128)(2,1)S(1)} %all-gather.5), channel_id=1, replica_groups=mesh['batch_0'=4,'batch_1'=4,'batch_2'=8,'mp_0'=2,'mp_1'=2] {'batch_2'}, dimensions={0}, use_global_device_ids=true | all-gather | bytes 248832 | tf_op jit(solution)/shard_map/all_gather | solution.py:22
  103.6 11.8 %all_gather.37 = bf16[128,12,288]{2,0,1:T(8,128)(2,1)S(1)} all-gather(bf16[32,12,288]{2,0,1:T(8,128)(2,1)S(1)} %copy.28), channel_id=1, replica_groups=mesh['batch_0'=4,'batch_1'=4,'batch_2'=8,'mp_0'=2,'mp_1'=2] {'batch_0'}, dimensions={0}, use_global_device_ids=true | all-gather | bytes 1105920 | tf_op jit(solution)/shard_map/all_gather | solution.py:22
  117.5 7.2 %all-gather.3 = bf16[32,288]{1,0:T(8,128)(2,1)S(1)} all-gather(bf16[16,288]{1,0:T(8,128)(2,1)S(1)} %convolution_convert_fusion), channel_id=5, replica_groups=mesh['batch_0'=4,'batch_1'=4,'batch_2'=8,'mp_0'=2,'mp_1'=2] {'mp_0'}, dimensions={0}, use_global_device_ids=true | all-gather | bytes 27648 | tf_op jit(solution)/shard_map/all_gather | solution.py:22
  124.7 14.2 %all_gather.39 = bf16[4,16,288]{2,1,0:T(8,128)(2,1)S(1)} all-gather(bf16[2,16,288]{2,1,0:T(8,128)(2,1)S(1)} %bitcast.75), channel_id=1, replica_groups=mesh['batch_0'=4,'batch_1'=4,'batch_2'=8,'mp_0'=2,'mp_1'=2] {'mp_1'}, dimensions={0}, use_global_device_ids=true | all-gather | bytes 55296 | tf_op jit(solution)/shard_map/all_gather | solution.py:22
  140.0 215.3 %while.40 = (s32[]{:T(128)}, bf16[4,1152]{1,0:T(4,128)(2,1)S(1)}, f32[4,1152]{1,0:T(4,128)S(1)}, f32[16,1152]{1,0:T(8,128)S(1)}, s32[16]{0:T(128)S(1)}, /*index=...) while((s32[]{:T(128)}, bf16[4,1152]{1,0:T(4,128)(2,1)S(1)}, ...), condition=%wide.region_3.4_spmd.clone, body=%wide.region_2.3_spmd.clone.sunk | while | flops 484565 | bytes 406372 | solution.py:124
  140.0 2.9 collective-permute-start
  146.0 4.4 collective-permute-done
  150.4 3.9 collective-permute-done.1
  159.4 5.4 collective-permute-done
  164.8 3.0 collective-permute-done.1
  172.8 5.4 collective-permute-done
  178.2 3.0 collective-permute-done.1
  186.2 5.4 collective-permute-done
  191.6 3.0 collective-permute-done.1
  199.6 5.4 collective-permute-done
  205.0 3.0 collective-permute-done.1
  213.0 5.4 collective-permute-done
  218.4 3.0 collective-permute-done.1
  226.4 5.4 collective-permute-done
  231.8 3.0 collective-permute-done.1
  239.7 5.4 collective-permute-done
  245.2 3.0 collective-permute-done.1
  253.1 5.4 collective-permute-done
  258.5 3.0 collective-permute-done.1
  266.5 5.6 collective-permute-done
  272.1 2.8 collective-permute-done.1
  279.9 5.4 collective-permute-done
  285.3 3.0 collective-permute-done.1
  293.3 5.4 collective-permute-done
  298.7 3.0 collective-permute-done.1
  306.7 5.4 collective-permute-done
  312.1 3.0 collective-permute-done.1
  320.1 5.4 collective-permute-done
  325.5 3.0 collective-permute-done.1
  333.5 5.4 collective-permute-done
  338.9 3.0 collective-permute-done.1
  346.9 5.4 collective-permute-done
  352.3 3.0 collective-permute-done.1
  355.3 196.7 %while.41 = (s32[]{:T(128)}, bf16[4,1152]{1,0:T(4,128)(2,1)S(1)}, f32[4,1152]{1,0:T(4,128)S(1)}, f32[16,1152]{1,0:T(8,128)S(1)}, s32[16]{0:T(128)S(1)}, /*index=...) while((s32[]{:T(128)}, bf16[4,1152]{1,0:T(4,128)(2,1)S(1)}, ...), condition=%wide.region_5.6_spmd.clone, body=%wide.region_4.5_spmd.clone.sunk | while | flops 470742 | bytes 443248 | solution.py:127
  355.3 3.4 collective-permute-start.2
  363.3 7.9 %collective-permute-start.2 = (bf16[4,1152]{1,0:T(4,128)(2,1)S(1)}, bf16[4,1152]{1,0:T(4,128)(2,1)S(1)}, u32[]{:S(2)}, u32[]{:S(2)}) collective-permute-start(bf16[4,1152]{1,0:T(4,128)(2,1)S(1)} %get-tuple-element.787), channel_id=1, source_target_pairs={{0,508},{4,0},{8,4},{12,8},{16,12},{20,16},{24,20},{28,24},{32,28}... | collective-permute-start | bytes 27656 | tf_op jit(solution)/shard_map/while/body/eval_jaxpr/ppermute | solution.py:36
  375.8 7.9 %collective-permute-start.2 = (bf16[4,1152]{1,0:T(4,128)(2,1)S(1)}, bf16[4,1152]{1,0:T(4,128)(2,1)S(1)}, u32[]{:S(2)}, u32[]{:S(2)}) collective-permute-start(bf16[4,1152]{1,0:T(4,128)(2,1)S(1)} %get-tuple-element.787), channel_id=1, source_target_pairs={{0,508},{4,0},{8,4},{12,8},{16,12},{20,16},{24,20},{28,24},{32,28}... | collective-permute-start | bytes 27656 | tf_op jit(solution)/shard_map/while/body/eval_jaxpr/ppermute | solution.py:36
  388.4 7.9 %collective-permute-start.2 = (bf16[4,1152]{1,0:T(4,128)(2,1)S(1)}, bf16[4,1152]{1,0:T(4,128)(2,1)S(1)}, u32[]{:S(2)}, u32[]{:S(2)}) collective-permute-start(bf16[4,1152]{1,0:T(4,128)(2,1)S(1)} %get-tuple-element.787), channel_id=1, source_target_pairs={{0,508},{4,0},{8,4},{12,8},{16,12},{20,16},{24,20},{28,24},{32,28}... | collective-permute-start | bytes 27656 | tf_op jit(solution)/shard_map/while/body/eval_jaxpr/ppermute | solution.py:36
  401.0 7.9 %collective-permute-start.2 = (bf16[4,1152]{1,0:T(4,128)(2,1)S(1)}, bf16[4,1152]{1,0:T(4,128)(2,1)S(1)}, u32[]{:S(2)}, u32[]{:S(2)}) collective-permute-start(bf16[4,1152]{1,0:T(4,128)(2,1)S(1)} %get-tuple-element.787), channel_id=1, source_target_pairs={{0,508},{4,0},{8,4},{12,8},{16,12},{20,16},{24,20},{28,24},{32,28}... | collective-permute-start | bytes 27656 | tf_op jit(solution)/shard_map/while/body/eval_jaxpr/ppermute | solution.py:36
  413.6 7.9 %collective-permute-start.2 = (bf16[4,1152]{1,0:T(4,128)(2,1)S(1)}, bf16[4,1152]{1,0:T(4,128)(2,1)S(1)}, u32[]{:S(2)}, u32[]{:S(2)}) collective-permute-start(bf16[4,1152]{1,0:T(4,128)(2,1)S(1)} %get-tuple-element.787), channel_id=1, source_target_pairs={{0,508},{4,0},{8,4},{12,8},{16,12},{20,16},{24,20},{28,24},{32,28}... | collective-permute-start | bytes 27656 | tf_op jit(solution)/shard_map/while/body/eval_jaxpr/ppermute | solution.py:36
  426.2 7.9 %collective-permute-start.2 = (bf16[4,1152]{1,0:T(4,128)(2,1)S(1)}, bf16[4,1152]{1,0:T(4,128)(2,1)S(1)}, u32[]{:S(2)}, u32[]{:S(2)}) collective-permute-start(bf16[4,1152]{1,0:T(4,128)(2,1)S(1)} %get-tuple-element.787), channel_id=1, source_target_pairs={{0,508},{4,0},{8,4},{12,8},{16,12},{20,16},{24,20},{28,24},{32,28}... | collective-permute-start | bytes 27656 | tf_op jit(solution)/shard_map/while/body/eval_jaxpr/ppermute | solution.py:36
  438.8 7.9 %collective-permute-start.2 = (bf16[4,1152]{1,0:T(4,128)(2,1)S(1)}, bf16[4,1152]{1,0:T(4,128)(2,1)S(1)}, u32[]{:S(2)}, u32[]{:S(2)}) collective-permute-start(bf16[4,1152]{1,0:T(4,128)(2,1)S(1)} %get-tuple-element.787), channel_id=1, source_target_pairs={{0,508},{4,0},{8,4},{12,8},{16,12},{20,16},{24,20},{28,24},{32,28}... | collective-permute-start | bytes 27656 | tf_op jit(solution)/shard_map/while/body/eval_jaxpr/ppermute | solution.py:36
  451.3 7.9 %collective-permute-start.2 = (bf16[4,1152]{1,0:T(4,128)(2,1)S(1)}, bf16[4,1152]{1,0:T(4,128)(2,1)S(1)}, u32[]{:S(2)}, u32[]{:S(2)}) collective-permute-start(bf16[4,1152]{1,0:T(4,128)(2,1)S(1)} %get-tuple-element.787), channel_id=1, source_target_pairs={{0,508},{4,0},{8,4},{12,8},{16,12},{20,16},{24,20},{28,24},{32,28}... | collective-permute-start | bytes 27656 | tf_op jit(solution)/shard_map/while/body/eval_jaxpr/ppermute | solution.py:36
  463.9 7.9 %collective-permute-start.2 = (bf16[4,1152]{1,0:T(4,128)(2,1)S(1)}, bf16[4,1152]{1,0:T(4,128)(2,1)S(1)}, u32[]{:S(2)}, u32[]{:S(2)}) collective-permute-start(bf16[4,1152]{1,0:T(4,128)(2,1)S(1)} %get-tuple-element.787), channel_id=1, source_target_pairs={{0,508},{4,0},{8,4},{12,8},{16,12},{20,16},{24,20},{28,24},{32,28}... | collective-permute-start | bytes 27656 | tf_op jit(solution)/shard_map/while/body/eval_jaxpr/ppermute | solution.py:36
  476.5 7.9 %collective-permute-start.2 = (bf16[4,1152]{1,0:T(4,128)(2,1)S(1)}, bf16[4,1152]{1,0:T(4,128)(2,1)S(1)}, u32[]{:S(2)}, u32[]{:S(2)}) collective-permute-start(bf16[4,1152]{1,0:T(4,128)(2,1)S(1)} %get-tuple-element.787), channel_id=1, source_target_pairs={{0,508},{4,0},{8,4},{12,8},{16,12},{20,16},{24,20},{28,24},{32,28}... | collective-permute-start | bytes 27656 | tf_op jit(solution)/shard_map/while/body/eval_jaxpr/ppermute | solution.py:36
  489.1 7.9 %collective-permute-start.2 = (bf16[4,1152]{1,0:T(4,128)(2,1)S(1)}, bf16[4,1152]{1,0:T(4,128)(2,1)S(1)}, u32[]{:S(2)}, u32[]{:S(2)}) collective-permute-start(bf16[4,1152]{1,0:T(4,128)(2,1)S(1)} %get-tuple-element.787), channel_id=1, source_target_pairs={{0,508},{4,0},{8,4},{12,8},{16,12},{20,16},{24,20},{28,24},{32,28}... | collective-permute-start | bytes 27656 | tf_op jit(solution)/shard_map/while/body/eval_jaxpr/ppermute | solution.py:36
  501.7 7.9 %collective-permute-start.2 = (bf16[4,1152]{1,0:T(4,128)(2,1)S(1)}, bf16[4,1152]{1,0:T(4,128)(2,1)S(1)}, u32[]{:S(2)}, u32[]{:S(2)}) collective-permute-start(bf16[4,1152]{1,0:T(4,128)(2,1)S(1)} %get-tuple-element.787), channel_id=1, source_target_pairs={{0,508},{4,0},{8,4},{12,8},{16,12},{20,16},{24,20},{28,24},{32,28}... | collective-permute-start | bytes 27656 | tf_op jit(solution)/shard_map/while/body/eval_jaxpr/ppermute | solution.py:36
  514.2 7.9 %collective-permute-start.2 = (bf16[4,1152]{1,0:T(4,128)(2,1)S(1)}, bf16[4,1152]{1,0:T(4,128)(2,1)S(1)}, u32[]{:S(2)}, u32[]{:S(2)}) collective-permute-start(bf16[4,1152]{1,0:T(4,128)(2,1)S(1)} %get-tuple-element.787), channel_id=1, source_target_pairs={{0,508},{4,0},{8,4},{12,8},{16,12},{20,16},{24,20},{28,24},{32,28}... | collective-permute-start | bytes 27656 | tf_op jit(solution)/shard_map/while/body/eval_jaxpr/ppermute | solution.py:36
  526.8 7.9 %collective-permute-start.2 = (bf16[4,1152]{1,0:T(4,128)(2,1)S(1)}, bf16[4,1152]{1,0:T(4,128)(2,1)S(1)}, u32[]{:S(2)}, u32[]{:S(2)}) collective-permute-start(bf16[4,1152]{1,0:T(4,128)(2,1)S(1)} %get-tuple-element.787), channel_id=1, source_target_pairs={{0,508},{4,0},{8,4},{12,8},{16,12},{20,16},{24,20},{28,24},{32,28}... | collective-permute-start | bytes 27656 | tf_op jit(solution)/shard_map/while/body/eval_jaxpr/ppermute | solution.py:36
  539.4 7.9 %collective-permute-start.2 = (bf16[4,1152]{1,0:T(4,128)(2,1)S(1)}, bf16[4,1152]{1,0:T(4,128)(2,1)S(1)}, u32[]{:S(2)}, u32[]{:S(2)}) collective-permute-start(bf16[4,1152]{1,0:T(4,128)(2,1)S(1)} %get-tuple-element.787), channel_id=1, source_target_pairs={{0,508},{4,0},{8,4},{12,8},{16,12},{20,16},{24,20},{28,24},{32,28}... | collective-permute-start | bytes 27656 | tf_op jit(solution)/shard_map/while/body/eval_jaxpr/ppermute | solution.py:36
  553.9 6.4 %collective-permute-start.4 = (f32[4,1152]{1,0:T(4,128)S(1)}, f32[4,1152]{1,0:T(4,128)S(1)}, u32[]{:S(2)}, u32[]{:S(2)}) collective-permute-start(f32[4,1152]{1,0:T(4,128)S(1)} %get-tuple-element.496), channel_id=1, source_target_pairs={{0,448},{4,452},{8,456},{12,460},{16,464},{20,468},{24,472},{28,47... | collective-permute-start | bytes 55304 | tf_op jit(solution)/shard_map/ppermute | solution.py:36
  561.1 45.8 %all-to-all-start = ((f32[4,16,288]{2,1,0:T(8,128)}), f32[4,16,288]{2,1,0:T(8,128)S(1)}, u32[]{:S(2)}, u32[]{:S(2)}) async-start(f32[4,16,288]{2,1,0:T(8,128)} %copy.32), calls=%async_computation | async-start | bytes 196608 | tf_op jit(solution)/shard_map/all_to_all | solution.py:46
  607.5 6.6 %all-to-all-done = f32[4,16,288]{2,1,0:T(8,128)S(1)} async-done(((f32[4,16,288]{2,1,0:T(8,128)}), f32[4,16,288]{2,1,0:T(8,128)S(1)}, u32[]{:S(2)}, u32[]{:S(2)}) %all-to-all-start) | async-done | bytes 73760 | tf_op jit(solution)/shard_map/all_to_all | solution.py:46
  (303 shorter events, 159.3 us)
Async XLA Ops:
  140.0 10.4 %collective-permute-start = (bf16[4,1152]{1,0:T(4,128)(2,1)S(1)}, bf16[4,1152]{1,0:T(4,128)(2,1)S(1)}, u32[]{:S(2)}, u32[]{:S(2)}) collective-permute-start(bf16[4,1152]{1,0:T(4,128)(2,1)S(1)} %copy.38), channel_id=1, source_target_pairs={{0,4},{4,8},{8,12},{12,16},{16,20},{20,24},{24,28},{28,32},{32,36}... | collective-permute-start | bytes 27656 | tf_op jit(solution)/shard_map/while/body/eval_jaxpr/ppermute | solution.py:36
  143.9 10.5 %collective-permute-start.1 = (f32[4,1152]{1,0:T(4,128)S(1)}, f32[4,1152]{1,0:T(4,128)S(1)}, u32[]{:S(2)}, u32[]{:S(2)}) collective-permute-start(f32[4,1152]{1,0:T(4,128)S(1)} %convolution_add_fusion.8), channel_id=1, source_target_pairs={{0,4},{4,8},{8,12},{12,16},{16,20},{20,24},{24,28},{28,32},{32,36}... | collective-permute-start | bytes 55304 | tf_op jit(solution)/shard_map/while/body/eval_jaxpr/ppermute | solution.py:36
  154.4 10.4 %collective-permute-start = (bf16[4,1152]{1,0:T(4,128)(2,1)S(1)}, bf16[4,1152]{1,0:T(4,128)(2,1)S(1)}, u32[]{:S(2)}, u32[]{:S(2)}) collective-permute-start(bf16[4,1152]{1,0:T(4,128)(2,1)S(1)} %copy.38), channel_id=1, source_target_pairs={{0,4},{4,8},{8,12},{12,16},{16,20},{20,24},{24,28},{28,32},{32,36}... | collective-permute-start | bytes 27656 | tf_op jit(solution)/shard_map/while/body/eval_jaxpr/ppermute | solution.py:36
  157.3 10.5 %collective-permute-start.1 = (f32[4,1152]{1,0:T(4,128)S(1)}, f32[4,1152]{1,0:T(4,128)S(1)}, u32[]{:S(2)}, u32[]{:S(2)}) collective-permute-start(f32[4,1152]{1,0:T(4,128)S(1)} %convolution_add_fusion.8), channel_id=1, source_target_pairs={{0,4},{4,8},{8,12},{12,16},{16,20},{20,24},{24,28},{28,32},{32,36}... | collective-permute-start | bytes 55304 | tf_op jit(solution)/shard_map/while/body/eval_jaxpr/ppermute | solution.py:36
  167.8 10.4 %collective-permute-start = (bf16[4,1152]{1,0:T(4,128)(2,1)S(1)}, bf16[4,1152]{1,0:T(4,128)(2,1)S(1)}, u32[]{:S(2)}, u32[]{:S(2)}) collective-permute-start(bf16[4,1152]{1,0:T(4,128)(2,1)S(1)} %copy.38), channel_id=1, source_target_pairs={{0,4},{4,8},{8,12},{12,16},{16,20},{20,24},{24,28},{28,32},{32,36}... | collective-permute-start | bytes 27656 | tf_op jit(solution)/shard_map/while/body/eval_jaxpr/ppermute | solution.py:36
  170.7 10.5 %collective-permute-start.1 = (f32[4,1152]{1,0:T(4,128)S(1)}, f32[4,1152]{1,0:T(4,128)S(1)}, u32[]{:S(2)}, u32[]{:S(2)}) collective-permute-start(f32[4,1152]{1,0:T(4,128)S(1)} %convolution_add_fusion.8), channel_id=1, source_target_pairs={{0,4},{4,8},{8,12},{12,16},{16,20},{20,24},{24,28},{28,32},{32,36}... | collective-permute-start | bytes 55304 | tf_op jit(solution)/shard_map/while/body/eval_jaxpr/ppermute | solution.py:36
  181.2 10.4 %collective-permute-start = (bf16[4,1152]{1,0:T(4,128)(2,1)S(1)}, bf16[4,1152]{1,0:T(4,128)(2,1)S(1)}, u32[]{:S(2)}, u32[]{:S(2)}) collective-permute-start(bf16[4,1152]{1,0:T(4,128)(2,1)S(1)} %copy.38), channel_id=1, source_target_pairs={{0,4},{4,8},{8,12},{12,16},{16,20},{20,24},{24,28},{28,32},{32,36}... | collective-permute-start | bytes 27656 | tf_op jit(solution)/shard_map/while/body/eval_jaxpr/ppermute | solution.py:36
  184.0 10.5 %collective-permute-start.1 = (f32[4,1152]{1,0:T(4,128)S(1)}, f32[4,1152]{1,0:T(4,128)S(1)}, u32[]{:S(2)}, u32[]{:S(2)}) collective-permute-start(f32[4,1152]{1,0:T(4,128)S(1)} %convolution_add_fusion.8), channel_id=1, source_target_pairs={{0,4},{4,8},{8,12},{12,16},{16,20},{20,24},{24,28},{28,32},{32,36}... | collective-permute-start | bytes 55304 | tf_op jit(solution)/shard_map/while/body/eval_jaxpr/ppermute | solution.py:36
  194.6 10.4 %collective-permute-start = (bf16[4,1152]{1,0:T(4,128)(2,1)S(1)}, bf16[4,1152]{1,0:T(4,128)(2,1)S(1)}, u32[]{:S(2)}, u32[]{:S(2)}) collective-permute-start(bf16[4,1152]{1,0:T(4,128)(2,1)S(1)} %copy.38), channel_id=1, source_target_pairs={{0,4},{4,8},{8,12},{12,16},{16,20},{20,24},{24,28},{28,32},{32,36}... | collective-permute-start | bytes 27656 | tf_op jit(solution)/shard_map/while/body/eval_jaxpr/ppermute | solution.py:36
  197.4 10.5 %collective-permute-start.1 = (f32[4,1152]{1,0:T(4,128)S(1)}, f32[4,1152]{1,0:T(4,128)S(1)}, u32[]{:S(2)}, u32[]{:S(2)}) collective-permute-start(f32[4,1152]{1,0:T(4,128)S(1)} %convolution_add_fusion.8), channel_id=1, source_target_pairs={{0,4},{4,8},{8,12},{12,16},{16,20},{20,24},{24,28},{28,32},{32,36}... | collective-permute-start | bytes 55304 | tf_op jit(solution)/shard_map/while/body/eval_jaxpr/ppermute | solution.py:36
  208.0 10.4 %collective-permute-start = (bf16[4,1152]{1,0:T(4,128)(2,1)S(1)}, bf16[4,1152]{1,0:T(4,128)(2,1)S(1)}, u32[]{:S(2)}, u32[]{:S(2)}) collective-permute-start(bf16[4,1152]{1,0:T(4,128)(2,1)S(1)} %copy.38), channel_id=1, source_target_pairs={{0,4},{4,8},{8,12},{12,16},{16,20},{20,24},{24,28},{28,32},{32,36}... | collective-permute-start | bytes 27656 | tf_op jit(solution)/shard_map/while/body/eval_jaxpr/ppermute | solution.py:36
  210.8 10.5 %collective-permute-start.1 = (f32[4,1152]{1,0:T(4,128)S(1)}, f32[4,1152]{1,0:T(4,128)S(1)}, u32[]{:S(2)}, u32[]{:S(2)}) collective-permute-start(f32[4,1152]{1,0:T(4,128)S(1)} %convolution_add_fusion.8), channel_id=1, source_target_pairs={{0,4},{4,8},{8,12},{12,16},{16,20},{20,24},{24,28},{28,32},{32,36}... | collective-permute-start | bytes 55304 | tf_op jit(solution)/shard_map/while/body/eval_jaxpr/ppermute | solution.py:36
  221.4 10.4 %collective-permute-start = (bf16[4,1152]{1,0:T(4,128)(2,1)S(1)}, bf16[4,1152]{1,0:T(4,128)(2,1)S(1)}, u32[]{:S(2)}, u32[]{:S(2)}) collective-permute-start(bf16[4,1152]{1,0:T(4,128)(2,1)S(1)} %copy.38), channel_id=1, source_target_pairs={{0,4},{4,8},{8,12},{12,16},{16,20},{20,24},{24,28},{28,32},{32,36}... | collective-permute-start | bytes 27656 | tf_op jit(solution)/shard_map/while/body/eval_jaxpr/ppermute | solution.py:36
  224.2 10.5 %collective-permute-start.1 = (f32[4,1152]{1,0:T(4,128)S(1)}, f32[4,1152]{1,0:T(4,128)S(1)}, u32[]{:S(2)}, u32[]{:S(2)}) collective-permute-start(f32[4,1152]{1,0:T(4,128)S(1)} %convolution_add_fusion.8), channel_id=1, source_target_pairs={{0,4},{4,8},{8,12},{12,16},{16,20},{20,24},{24,28},{28,32},{32,36}... | collective-permute-start | bytes 55304 | tf_op jit(solution)/shard_map/while/body/eval_jaxpr/ppermute | solution.py:36
  234.7 10.4 %collective-permute-start = (bf16[4,1152]{1,0:T(4,128)(2,1)S(1)}, bf16[4,1152]{1,0:T(4,128)(2,1)S(1)}, u32[]{:S(2)}, u32[]{:S(2)}) collective-permute-start(bf16[4,1152]{1,0:T(4,128)(2,1)S(1)} %copy.38), channel_id=1, source_target_pairs={{0,4},{4,8},{8,12},{12,16},{16,20},{20,24},{24,28},{28,32},{32,36}... | collective-permute-start | bytes 27656 | tf_op jit(solution)/shard_map/while/body/eval_jaxpr/ppermute | solution.py:36
  237.6 10.5 %collective-permute-start.1 = (f32[4,1152]{1,0:T(4,128)S(1)}, f32[4,1152]{1,0:T(4,128)S(1)}, u32[]{:S(2)}, u32[]{:S(2)}) collective-permute-start(f32[4,1152]{1,0:T(4,128)S(1)} %convolution_add_fusion.8), channel_id=1, source_target_pairs={{0,4},{4,8},{8,12},{12,16},{16,20},{20,24},{24,28},{28,32},{32,36}... | collective-permute-start | bytes 55304 | tf_op jit(solution)/shard_map/while/body/eval_jaxpr/ppermute | solution.py:36
  248.1 10.4 %collective-permute-start = (bf16[4,1152]{1,0:T(4,128)(2,1)S(1)}, bf16[4,1152]{1,0:T(4,128)(2,1)S(1)}, u32[]{:S(2)}, u32[]{:S(2)}) collective-permute-start(bf16[4,1152]{1,0:T(4,128)(2,1)S(1)} %copy.38), channel_id=1, source_target_pairs={{0,4},{4,8},{8,12},{12,16},{16,20},{20,24},{24,28},{28,32},{32,36}... | collective-permute-start | bytes 27656 | tf_op jit(solution)/shard_map/while/body/eval_jaxpr/ppermute | solution.py:36
  251.0 10.5 %collective-permute-start.1 = (f32[4,1152]{1,0:T(4,128)S(1)}, f32[4,1152]{1,0:T(4,128)S(1)}, u32[]{:S(2)}, u32[]{:S(2)}) collective-permute-start(f32[4,1152]{1,0:T(4,128)S(1)} %convolution_add_fusion.8), channel_id=1, source_target_pairs={{0,4},{4,8},{8,12},{12,16},{16,20},{20,24},{24,28},{28,32},{32,36}... | collective-permute-start | bytes 55304 | tf_op jit(solution)/shard_map/while/body/eval_jaxpr/ppermute | solution.py:36
  261.5 10.6 %collective-permute-start = (bf16[4,1152]{1,0:T(4,128)(2,1)S(1)}, bf16[4,1152]{1,0:T(4,128)(2,1)S(1)}, u32[]{:S(2)}, u32[]{:S(2)}) collective-permute-start(bf16[4,1152]{1,0:T(4,128)(2,1)S(1)} %copy.38), channel_id=1, source_target_pairs={{0,4},{4,8},{8,12},{12,16},{16,20},{20,24},{24,28},{28,32},{32,36}... | collective-permute-start | bytes 27656 | tf_op jit(solution)/shard_map/while/body/eval_jaxpr/ppermute | solution.py:36
  264.4 10.5 %collective-permute-start.1 = (f32[4,1152]{1,0:T(4,128)S(1)}, f32[4,1152]{1,0:T(4,128)S(1)}, u32[]{:S(2)}, u32[]{:S(2)}) collective-permute-start(f32[4,1152]{1,0:T(4,128)S(1)} %convolution_add_fusion.8), channel_id=1, source_target_pairs={{0,4},{4,8},{8,12},{12,16},{16,20},{20,24},{24,28},{28,32},{32,36}... | collective-permute-start | bytes 55304 | tf_op jit(solution)/shard_map/while/body/eval_jaxpr/ppermute | solution.py:36
  274.9 10.4 %collective-permute-start = (bf16[4,1152]{1,0:T(4,128)(2,1)S(1)}, bf16[4,1152]{1,0:T(4,128)(2,1)S(1)}, u32[]{:S(2)}, u32[]{:S(2)}) collective-permute-start(bf16[4,1152]{1,0:T(4,128)(2,1)S(1)} %copy.38), channel_id=1, source_target_pairs={{0,4},{4,8},{8,12},{12,16},{16,20},{20,24},{24,28},{28,32},{32,36}... | collective-permute-start | bytes 27656 | tf_op jit(solution)/shard_map/while/body/eval_jaxpr/ppermute | solution.py:36
  277.8 10.5 %collective-permute-start.1 = (f32[4,1152]{1,0:T(4,128)S(1)}, f32[4,1152]{1,0:T(4,128)S(1)}, u32[]{:S(2)}, u32[]{:S(2)}) collective-permute-start(f32[4,1152]{1,0:T(4,128)S(1)} %convolution_add_fusion.8), channel_id=1, source_target_pairs={{0,4},{4,8},{8,12},{12,16},{16,20},{20,24},{24,28},{28,32},{32,36}... | collective-permute-start | bytes 55304 | tf_op jit(solution)/shard_map/while/body/eval_jaxpr/ppermute | solution.py:36
  288.3 10.4 %collective-permute-start = (bf16[4,1152]{1,0:T(4,128)(2,1)S(1)}, bf16[4,1152]{1,0:T(4,128)(2,1)S(1)}, u32[]{:S(2)}, u32[]{:S(2)}) collective-permute-start(bf16[4,1152]{1,0:T(4,128)(2,1)S(1)} %copy.38), channel_id=1, source_target_pairs={{0,4},{4,8},{8,12},{12,16},{16,20},{20,24},{24,28},{28,32},{32,36}... | collective-permute-start | bytes 27656 | tf_op jit(solution)/shard_map/while/body/eval_jaxpr/ppermute | solution.py:36
  291.2 10.5 %collective-permute-start.1 = (f32[4,1152]{1,0:T(4,128)S(1)}, f32[4,1152]{1,0:T(4,128)S(1)}, u32[]{:S(2)}, u32[]{:S(2)}) collective-permute-start(f32[4,1152]{1,0:T(4,128)S(1)} %convolution_add_fusion.8), channel_id=1, source_target_pairs={{0,4},{4,8},{8,12},{12,16},{16,20},{20,24},{24,28},{28,32},{32,36}... | collective-permute-start | bytes 55304 | tf_op jit(solution)/shard_map/while/body/eval_jaxpr/ppermute | solution.py:36
  301.7 10.4 %collective-permute-start = (bf16[4,1152]{1,0:T(4,128)(2,1)S(1)}, bf16[4,1152]{1,0:T(4,128)(2,1)S(1)}, u32[]{:S(2)}, u32[]{:S(2)}) collective-permute-start(bf16[4,1152]{1,0:T(4,128)(2,1)S(1)} %copy.38), channel_id=1, source_target_pairs={{0,4},{4,8},{8,12},{12,16},{16,20},{20,24},{24,28},{28,32},{32,36}... | collective-permute-start | bytes 27656 | tf_op jit(solution)/shard_map/while/body/eval_jaxpr/ppermute | solution.py:36
  304.6 10.5 %collective-permute-start.1 = (f32[4,1152]{1,0:T(4,128)S(1)}, f32[4,1152]{1,0:T(4,128)S(1)}, u32[]{:S(2)}, u32[]{:S(2)}) collective-permute-start(f32[4,1152]{1,0:T(4,128)S(1)} %convolution_add_fusion.8), channel_id=1, source_target_pairs={{0,4},{4,8},{8,12},{12,16},{16,20},{20,24},{24,28},{28,32},{32,36}... | collective-permute-start | bytes 55304 | tf_op jit(solution)/shard_map/while/body/eval_jaxpr/ppermute | solution.py:36
  315.1 10.4 %collective-permute-start = (bf16[4,1152]{1,0:T(4,128)(2,1)S(1)}, bf16[4,1152]{1,0:T(4,128)(2,1)S(1)}, u32[]{:S(2)}, u32[]{:S(2)}) collective-permute-start(bf16[4,1152]{1,0:T(4,128)(2,1)S(1)} %copy.38), channel_id=1, source_target_pairs={{0,4},{4,8},{8,12},{12,16},{16,20},{20,24},{24,28},{28,32},{32,36}... | collective-permute-start | bytes 27656 | tf_op jit(solution)/shard_map/while/body/eval_jaxpr/ppermute | solution.py:36
  317.9 10.5 %collective-permute-start.1 = (f32[4,1152]{1,0:T(4,128)S(1)}, f32[4,1152]{1,0:T(4,128)S(1)}, u32[]{:S(2)}, u32[]{:S(2)}) collective-permute-start(f32[4,1152]{1,0:T(4,128)S(1)} %convolution_add_fusion.8), channel_id=1, source_target_pairs={{0,4},{4,8},{8,12},{12,16},{16,20},{20,24},{24,28},{28,32},{32,36}... | collective-permute-start | bytes 55304 | tf_op jit(solution)/shard_map/while/body/eval_jaxpr/ppermute | solution.py:36
  328.5 10.4 %collective-permute-start = (bf16[4,1152]{1,0:T(4,128)(2,1)S(1)}, bf16[4,1152]{1,0:T(4,128)(2,1)S(1)}, u32[]{:S(2)}, u32[]{:S(2)}) collective-permute-start(bf16[4,1152]{1,0:T(4,128)(2,1)S(1)} %copy.38), channel_id=1, source_target_pairs={{0,4},{4,8},{8,12},{12,16},{16,20},{20,24},{24,28},{28,32},{32,36}... | collective-permute-start | bytes 27656 | tf_op jit(solution)/shard_map/while/body/eval_jaxpr/ppermute | solution.py:36
  331.3 10.5 %collective-permute-start.1 = (f32[4,1152]{1,0:T(4,128)S(1)}, f32[4,1152]{1,0:T(4,128)S(1)}, u32[]{:S(2)}, u32[]{:S(2)}) collective-permute-start(f32[4,1152]{1,0:T(4,128)S(1)} %convolution_add_fusion.8), channel_id=1, source_target_pairs={{0,4},{4,8},{8,12},{12,16},{16,20},{20,24},{24,28},{28,32},{32,36}... | collective-permute-start | bytes 55304 | tf_op jit(solution)/shard_map/while/body/eval_jaxpr/ppermute | solution.py:36
  341.9 10.4 %collective-permute-start = (bf16[4,1152]{1,0:T(4,128)(2,1)S(1)}, bf16[4,1152]{1,0:T(4,128)(2,1)S(1)}, u32[]{:S(2)}, u32[]{:S(2)}) collective-permute-start(bf16[4,1152]{1,0:T(4,128)(2,1)S(1)} %copy.38), channel_id=1, source_target_pairs={{0,4},{4,8},{8,12},{12,16},{16,20},{20,24},{24,28},{28,32},{32,36}... | collective-permute-start | bytes 27656 | tf_op jit(solution)/shard_map/while/body/eval_jaxpr/ppermute | solution.py:36
  344.7 10.5 %collective-permute-start.1 = (f32[4,1152]{1,0:T(4,128)S(1)}, f32[4,1152]{1,0:T(4,128)S(1)}, u32[]{:S(2)}, u32[]{:S(2)}) collective-permute-start(f32[4,1152]{1,0:T(4,128)S(1)} %convolution_add_fusion.8), channel_id=1, source_target_pairs={{0,4},{4,8},{8,12},{12,16},{16,20},{20,24},{24,28},{28,32},{32,36}... | collective-permute-start | bytes 55304 | tf_op jit(solution)/shard_map/while/body/eval_jaxpr/ppermute | solution.py:36
  355.3 5.3 collective-permute-start.2
  358.6 4.5 collective-permute-start.3
  363.3 9.9 %collective-permute-start.2 = (bf16[4,1152]{1,0:T(4,128)(2,1)S(1)}, bf16[4,1152]{1,0:T(4,128)(2,1)S(1)}, u32[]{:S(2)}, u32[]{:S(2)}) collective-permute-start(bf16[4,1152]{1,0:T(4,128)(2,1)S(1)} %get-tuple-element.787), channel_id=1, source_target_pairs={{0,508},{4,0},{8,4},{12,8},{16,12},{20,16},{24,20},{28,24},{32,28}... | collective-permute-start | bytes 27656 | tf_op jit(solution)/shard_map/while/body/eval_jaxpr/ppermute | solution.py:36
  371.2 4.5 collective-permute-start.3
  375.8 9.9 %collective-permute-start.2 = (bf16[4,1152]{1,0:T(4,128)(2,1)S(1)}, bf16[4,1152]{1,0:T(4,128)(2,1)S(1)}, u32[]{:S(2)}, u32[]{:S(2)}) collective-permute-start(bf16[4,1152]{1,0:T(4,128)(2,1)S(1)} %get-tuple-element.787), channel_id=1, source_target_pairs={{0,508},{4,0},{8,4},{12,8},{16,12},{20,16},{24,20},{28,24},{32,28}... | collective-permute-start | bytes 27656 | tf_op jit(solution)/shard_map/while/body/eval_jaxpr/ppermute | solution.py:36
  383.8 4.5 collective-permute-start.3
  388.4 9.9 %collective-permute-start.2 = (bf16[4,1152]{1,0:T(4,128)(2,1)S(1)}, bf16[4,1152]{1,0:T(4,128)(2,1)S(1)}, u32[]{:S(2)}, u32[]{:S(2)}) collective-permute-start(bf16[4,1152]{1,0:T(4,128)(2,1)S(1)} %get-tuple-element.787), channel_id=1, source_target_pairs={{0,508},{4,0},{8,4},{12,8},{16,12},{20,16},{24,20},{28,24},{32,28}... | collective-permute-start | bytes 27656 | tf_op jit(solution)/shard_map/while/body/eval_jaxpr/ppermute | solution.py:36
  396.4 4.5 collective-permute-start.3
  401.0 9.9 %collective-permute-start.2 = (bf16[4,1152]{1,0:T(4,128)(2,1)S(1)}, bf16[4,1152]{1,0:T(4,128)(2,1)S(1)}, u32[]{:S(2)}, u32[]{:S(2)}) collective-permute-start(bf16[4,1152]{1,0:T(4,128)(2,1)S(1)} %get-tuple-element.787), channel_id=1, source_target_pairs={{0,508},{4,0},{8,4},{12,8},{16,12},{20,16},{24,20},{28,24},{32,28}... | collective-permute-start | bytes 27656 | tf_op jit(solution)/shard_map/while/body/eval_jaxpr/ppermute | solution.py:36
  409.0 4.5 collective-permute-start.3
  413.6 9.9 %collective-permute-start.2 = (bf16[4,1152]{1,0:T(4,128)(2,1)S(1)}, bf16[4,1152]{1,0:T(4,128)(2,1)S(1)}, u32[]{:S(2)}, u32[]{:S(2)}) collective-permute-start(bf16[4,1152]{1,0:T(4,128)(2,1)S(1)} %get-tuple-element.787), channel_id=1, source_target_pairs={{0,508},{4,0},{8,4},{12,8},{16,12},{20,16},{24,20},{28,24},{32,28}... | collective-permute-start | bytes 27656 | tf_op jit(solution)/shard_map/while/body/eval_jaxpr/ppermute | solution.py:36
  421.5 4.5 collective-permute-start.3
  426.2 9.9 %collective-permute-start.2 = (bf16[4,1152]{1,0:T(4,128)(2,1)S(1)}, bf16[4,1152]{1,0:T(4,128)(2,1)S(1)}, u32[]{:S(2)}, u32[]{:S(2)}) collective-permute-start(bf16[4,1152]{1,0:T(4,128)(2,1)S(1)} %get-tuple-element.787), channel_id=1, source_target_pairs={{0,508},{4,0},{8,4},{12,8},{16,12},{20,16},{24,20},{28,24},{32,28}... | collective-permute-start | bytes 27656 | tf_op jit(solution)/shard_map/while/body/eval_jaxpr/ppermute | solution.py:36
  434.1 4.5 collective-permute-start.3
  438.8 9.9 %collective-permute-start.2 = (bf16[4,1152]{1,0:T(4,128)(2,1)S(1)}, bf16[4,1152]{1,0:T(4,128)(2,1)S(1)}, u32[]{:S(2)}, u32[]{:S(2)}) collective-permute-start(bf16[4,1152]{1,0:T(4,128)(2,1)S(1)} %get-tuple-element.787), channel_id=1, source_target_pairs={{0,508},{4,0},{8,4},{12,8},{16,12},{20,16},{24,20},{28,24},{32,28}... | collective-permute-start | bytes 27656 | tf_op jit(solution)/shard_map/while/body/eval_jaxpr/ppermute | solution.py:36
  446.7 4.5 collective-permute-start.3
  451.3 9.9 %collective-permute-start.2 = (bf16[4,1152]{1,0:T(4,128)(2,1)S(1)}, bf16[4,1152]{1,0:T(4,128)(2,1)S(1)}, u32[]{:S(2)}, u32[]{:S(2)}) collective-permute-start(bf16[4,1152]{1,0:T(4,128)(2,1)S(1)} %get-tuple-element.787), channel_id=1, source_target_pairs={{0,508},{4,0},{8,4},{12,8},{16,12},{20,16},{24,20},{28,24},{32,28}... | collective-permute-start | bytes 27656 | tf_op jit(solution)/shard_map/while/body/eval_jaxpr/ppermute | solution.py:36
  459.3 4.5 collective-permute-start.3
  463.9 9.9 %collective-permute-start.2 = (bf16[4,1152]{1,0:T(4,128)(2,1)S(1)}, bf16[4,1152]{1,0:T(4,128)(2,1)S(1)}, u32[]{:S(2)}, u32[]{:S(2)}) collective-permute-start(bf16[4,1152]{1,0:T(4,128)(2,1)S(1)} %get-tuple-element.787), channel_id=1, source_target_pairs={{0,508},{4,0},{8,4},{12,8},{16,12},{20,16},{24,20},{28,24},{32,28}... | collective-permute-start | bytes 27656 | tf_op jit(solution)/shard_map/while/body/eval_jaxpr/ppermute | solution.py:36
  471.9 4.5 collective-permute-start.3
  476.5 9.9 %collective-permute-start.2 = (bf16[4,1152]{1,0:T(4,128)(2,1)S(1)}, bf16[4,1152]{1,0:T(4,128)(2,1)S(1)}, u32[]{:S(2)}, u32[]{:S(2)}) collective-permute-start(bf16[4,1152]{1,0:T(4,128)(2,1)S(1)} %get-tuple-element.787), channel_id=1, source_target_pairs={{0,508},{4,0},{8,4},{12,8},{16,12},{20,16},{24,20},{28,24},{32,28}... | collective-permute-start | bytes 27656 | tf_op jit(solution)/shard_map/while/body/eval_jaxpr/ppermute | solution.py:36
  484.5 4.5 collective-permute-start.3
  489.1 9.9 %collective-permute-start.2 = (bf16[4,1152]{1,0:T(4,128)(2,1)S(1)}, bf16[4,1152]{1,0:T(4,128)(2,1)S(1)}, u32[]{:S(2)}, u32[]{:S(2)}) collective-permute-start(bf16[4,1152]{1,0:T(4,128)(2,1)S(1)} %get-tuple-element.787), channel_id=1, source_target_pairs={{0,508},{4,0},{8,4},{12,8},{16,12},{20,16},{24,20},{28,24},{32,28}... | collective-permute-start | bytes 27656 | tf_op jit(solution)/shard_map/while/body/eval_jaxpr/ppermute | solution.py:36
  497.0 4.5 collective-permute-start.3
  501.7 9.9 %collective-permute-start.2 = (bf16[4,1152]{1,0:T(4,128)(2,1)S(1)}, bf16[4,1152]{1,0:T(4,128)(2,1)S(1)}, u32[]{:S(2)}, u32[]{:S(2)}) collective-permute-start(bf16[4,1152]{1,0:T(4,128)(2,1)S(1)} %get-tuple-element.787), channel_id=1, source_target_pairs={{0,508},{4,0},{8,4},{12,8},{16,12},{20,16},{24,20},{28,24},{32,28}... | collective-permute-start | bytes 27656 | tf_op jit(solution)/shard_map/while/body/eval_jaxpr/ppermute | solution.py:36
  514.2 9.9 %collective-permute-start.2 = (bf16[4,1152]{1,0:T(4,128)(2,1)S(1)}, bf16[4,1152]{1,0:T(4,128)(2,1)S(1)}, u32[]{:S(2)}, u32[]{:S(2)}) collective-permute-start(bf16[4,1152]{1,0:T(4,128)(2,1)S(1)} %get-tuple-element.787), channel_id=1, source_target_pairs={{0,508},{4,0},{8,4},{12,8},{16,12},{20,16},{24,20},{28,24},{32,28}... | collective-permute-start | bytes 27656 | tf_op jit(solution)/shard_map/while/body/eval_jaxpr/ppermute | solution.py:36
  526.8 9.9 %collective-permute-start.2 = (bf16[4,1152]{1,0:T(4,128)(2,1)S(1)}, bf16[4,1152]{1,0:T(4,128)(2,1)S(1)}, u32[]{:S(2)}, u32[]{:S(2)}) collective-permute-start(bf16[4,1152]{1,0:T(4,128)(2,1)S(1)} %get-tuple-element.787), channel_id=1, source_target_pairs={{0,508},{4,0},{8,4},{12,8},{16,12},{20,16},{24,20},{28,24},{32,28}... | collective-permute-start | bytes 27656 | tf_op jit(solution)/shard_map/while/body/eval_jaxpr/ppermute | solution.py:36
  539.4 9.9 %collective-permute-start.2 = (bf16[4,1152]{1,0:T(4,128)(2,1)S(1)}, bf16[4,1152]{1,0:T(4,128)(2,1)S(1)}, u32[]{:S(2)}, u32[]{:S(2)}) collective-permute-start(bf16[4,1152]{1,0:T(4,128)(2,1)S(1)} %get-tuple-element.787), channel_id=1, source_target_pairs={{0,508},{4,0},{8,4},{12,8},{16,12},{20,16},{24,20},{28,24},{32,28}... | collective-permute-start | bytes 27656 | tf_op jit(solution)/shard_map/while/body/eval_jaxpr/ppermute | solution.py:36
  547.4 4.5 collective-permute-start.3
  552.0 54.8 %collective-permute-start.5 = (f32[4,1152]{1,0:T(4,128)S(1)}, f32[4,1152]{1,0:T(4,128)S(1)}, u32[]{:S(2)}, u32[]{:S(2)}) collective-permute-start(f32[4,1152]{1,0:T(4,128)S(1)} %get-tuple-element.497), channel_id=1, source_target_pairs={{0,64},{4,68},{8,72},{12,76},{16,80},{20,84},{24,88},{28,92},{32,9... | collective-permute-start | bytes 55304 | tf_op jit(solution)/shard_map/ppermute | solution.py:36
  553.9 52.9 %collective-permute-start.4 = (f32[4,1152]{1,0:T(4,128)S(1)}, f32[4,1152]{1,0:T(4,128)S(1)}, u32[]{:S(2)}, u32[]{:S(2)}) collective-permute-start(f32[4,1152]{1,0:T(4,128)S(1)} %get-tuple-element.496), channel_id=1, source_target_pairs={{0,448},{4,452},{8,456},{12,460},{16,464},{20,468},{24,472},{28,47... | collective-permute-start | bytes 55304 | tf_op jit(solution)/shard_map/ppermute | solution.py:36
  561.1 53.0 %all-to-all-start = ((f32[4,16,288]{2,1,0:T(8,128)}), f32[4,16,288]{2,1,0:T(8,128)S(1)}, u32[]{:S(2)}, u32[]{:S(2)}) async-start(f32[4,16,288]{2,1,0:T(8,128)} %copy.32), calls=%async_computation | async-start | bytes 196608 | tf_op jit(solution)/shard_map/all_to_all | solution.py:46
  (10 other events, 390.7 us)
where the time goes:
time: 618 us; the launch traced here: 615 us
  starting transfers between devices  269 us (44%)
  waiting for transfers between devices  165 us (27%)
  blocking collectives  133 us (22%)
  matrix products  36.3 us (6%)
    ppermute x66, starting transfers between devices, from_behind(): return lax.ppermute(value, axis, pairs)  223 us
    ppermute x66, waiting for transfers between devices, from_behind(): return lax.ppermute(value, axis, pairs)  158 us
    all_gather x10, blocking collectives, stacked_from(): pieces = lax.all_gather(pieces, axes[k], axis=0, tiled=True)  133 us
    all_to_all x1, starting transfers between devices, sent_and_summed(): lax.all_to_all(pieces, axis, split_axis=0, concat_axis=0, tiled=True)  45.8 us
    dot_general x32, matrix products, block_update(): lax.dot_general(image, text, (((1,), (1,)), ((), ())), preferred_element_...  24.9 us
  transfers between devices with their start and end apart: 67, of which 49 were waited for; matrix products, arithmetic and copies ran while one was open for 6% of the time, Pallas kernels for 0%

commit v1 on v0

--- a/solution.py
+++ b/solution.py
@@ -19,7 +19,9 @@
 def stacked_from(x, axes, order):
     pieces = x[None]
     for k in order:
-        pieces = lax.all_gather(pieces, axes[k], axis=0, tiled=True)
+        pieces = jnp.concatenate(
+            lax.all_to_all(jnp.stack([pieces] * lax.axis_size(axes[k])), axes[k], 0, 0), axis=0
+        )
     current = [lax.axis_size(axes[k]) for k in reversed(order)]
     pieces = pieces.reshape(*current, *x.shape)
     turned = sorted(range(len(order)), key=lambda place: order[len(order) - 1 - place])

time: 618 us -> 599 us (0.969)
  blocking collectives: 133 us -> 27.6 us
  waiting for transfers between devices: 165 us -> 214 us
  starting transfers between devices: 269 us -> 297 us
  local copies, waits for them, and re-layouts: 4.98 us -> 12.4 us
    all_gather x10 -> x0, blocking collectives: 133 us -> none  [stacked_from(): pieces = lax.all_gather(pieces, axes[k], axis=0, tiled=True)]
    all_to_all x0 -> x7, waiting for transfers between devices: none -> 48.7 us  [stacked_from(): lax.all_to_all(jnp.stack([pieces] * lax.axis_size(axes[k])), axes[k], 0, 0)]
    all_to_all x0 -> x7, starting transfers between devices: none -> 32.3 us  [stacked_from(): lax.all_to_all(jnp.stack([pieces] * lax.axis_size(axes[k])), axes[k], 0, 0)]
    all_to_all x0 -> x3, blocking collectives: none -> 27.6 us  [stacked_from(): lax.all_to_all(jnp.stack([pieces] * lax.axis_size(axes[k])), axes[k], 0, 0)]
    another operation x0 -> x10, local copies, waits for them, and re-layouts: none -> 6.31 us  [stacked_from(): jnp.stack([pieces] * lax.axis_size(axes[k]))]
  transfers between devices with their start and end apart: 67 -> 74, of which waited for: 49 -> 56; matrix products, arithmetic and copies ran while one was open for 6% -> 7% of each run, Pallas kernels for 0% -> 0%
where the time goes in v1:
time: 599 us; the launch traced here: 595 us
  starting transfers between devices  297 us (50%)
  waiting for transfers between devices  214 us (36%)
  matrix products  37.5 us (6%)
  blocking collectives  27.6 us (5%)
  local copies, waits for them, and re-layouts  12.4 us (2%)
    ppermute x66, starting transfers between devices, from_behind(): return lax.ppermute(value, axis, pairs)  223 us
    ppermute x66, waiting for transfers between devices, from_behind(): return lax.ppermute(value, axis, pairs)  158 us
    all_to_all x7, waiting for transfers between devices, stacked_from(): lax.all_to_all(jnp.stack([pieces] * lax.axis_size(axes[k])), axes[k], 0, 0)  48.7 us
    all_to_all x1, starting transfers between devices, sent_and_summed(): lax.all_to_all(pieces, axis, split_axis=0, concat_axis=0, tiled=True)  42 us
    all_to_all x7, starting transfers between devices, stacked_from(): lax.all_to_all(jnp.stack([pieces] * lax.axis_size(axes[k])), axes[k], 0, 0)  32.3 us
    all_to_all x3, blocking collectives, stacked_from(): lax.all_to_all(jnp.stack([pieces] * lax.axis_size(axes[k])), axes[k], 0, 0)  27.6 us
    dot_general x32, matrix products, block_update(): lax.dot_general(image, text, (((1,), (1,)), ((), ())), preferred_element_...  24.8 us
  transfers between devices with their start and end apart: 74, of which 56 were waited for; matrix products, arithmetic and copies ran while one was open for 7% of the time, Pallas kernels for 0%

profile of v1, /device:TPU:1, one launch (start us, length us, event | category | flops | bytes accessed | tf_op | source)
XLA Modules:
  0.0 595.5 jit_solution(13718331269141001594)
XLA Ops:
  1.4 9.7 %all_to_all.55 = bf16[4,1,12,288]{3,2,1,0:T(8,128)(2,1)S(1)} all-to-all(bf16[4,1,12,288]{3,2,1,0:T(8,128)(2,1)S(1)} %stack.30), channel_id=1, replica_groups=mesh['batch_0'=4,'batch_1'=4,'batch_2'=8,'mp_0'=2,'mp_1'=2] {'batch_1'}, dimensions={0} | all-to-all | bytes 55296 | tf_op jit(solution)/shard_map/all_to_all | solution.py:23
  12.5 3.3 all-to-all-start.5
  15.8 4.5 all-to-all-done.5
  21.0 10.0 %all-to-all-start.1 = ((bf16[8,4,12,288]{3,1,2,0:T(4,128)(2,1)}), bf16[8,4,12,288]{3,1,2,0:T(4,128)(2,1)S(1)}, u32[]{:S(2)}, u32[]{:S(2)}) async-start(bf16[8,4,12,288]{3,1,2,0:T(4,128)(2,1)} %stack.31), calls=%async_computation.1 | async-start | bytes 589824 | tf_op jit(solution)/shard_map/all_to_all | solution.py:23
  31.1 9.8 %all-to-all-done.1 = bf16[8,4,12,288]{3,1,2,0:T(4,128)(2,1)S(1)} async-done(((bf16[8,4,12,288]{3,1,2,0:T(4,128)(2,1)}), bf16[8,4,12,288]{3,1,2,0:T(4,128)(2,1)S(1)}, u32[]{:S(2)}, u32[]{:S(2)}) %all-to-all-start.1) | async-done | bytes 221216 | tf_op jit(solution)/shard_map/all_to_all | solution.py:23
  41.7 3.4 all-to-all-start.6
  45.3 9.3 %all-to-all-done.6 = bf16[8,4,12,288]{3,1,2,0:T(4,128)(2,1)S(1)} async-done(((bf16[8,4,12,288]{3,1,2,0:T(4,128)(2,1)}), bf16[8,4,12,288]{3,1,2,0:T(4,128)(2,1)S(1)}, u32[]{:S(2)}, u32[]{:S(2)}) %all-to-all-start.6) | async-done | bytes 221216 | tf_op jit(solution)/shard_map/all_to_all | solution.py:23
  55.9 4.0 all-to-all-start.2
  60.1 10.2 %all-to-all-done.2 = bf16[4,32,12,288]{3,1,2,0:T(8,128)(2,1)S(1)} async-done(((bf16[4,32,12,288]{3,1,2,0:T(8,128)(2,1)}), bf16[4,32,12,288]{3,1,2,0:T(8,128)(2,1)S(1)}, u32[]{:S(2)}, u32[]{:S(2)}) %all-to-all-start.2) | async-done | bytes 884768 | tf_op jit(solution)/shard_map/all_to_all | solution.py:23
  71.5 3.5 all-to-all-start.7
  80.6 4.8 all-to-all-done.7
  85.5 4.8 all-to-all-start.3
  93.2 3.7 all-to-all-done.3
  96.9 12.9 %all_to_all.56 = bf16[2,2,16,288]{3,2,1,0:T(8,128)(2,1)S(1)} all-to-all(bf16[2,2,16,288]{3,2,1,0:T(8,128)(2,1)S(1)} %pad_maximum_fusion), channel_id=1, replica_groups=mesh['batch_0'=4,'batch_1'=4,'batch_2'=8,'mp_0'=2,'mp_1'=2] {'mp_1'}, dimensions={0} | all-to-all | bytes 73728 | tf_op jit(solution)/shard_map/all_to_all | solution.py:23
  109.9 3.2 all-to-all-start.8
  113.5 6.3 %all-to-all-done.8 = bf16[2,1,16,288]{3,2,1,0:T(8,128)(2,1)S(1)} async-done(((bf16[2,1,16,288]{3,2,1,0:T(8,128)(2,1)}), bf16[2,1,16,288]{3,2,1,0:T(8,128)(2,1)S(1)}, u32[]{:S(2)}, u32[]{:S(2)}) %all-to-all-start.8) | async-done | bytes 18464 | tf_op jit(solution)/shard_map/all_to_all | solution.py:23
  119.8 4.9 all_to_all.57
  125.1 214.7 %while.40 = (s32[]{:T(128)}, bf16[4,1152]{1,0:T(4,128)(2,1)S(1)}, f32[4,1152]{1,0:T(4,128)S(1)}, f32[16,1152]{1,0:T(8,128)S(1)}, s32[16]{0:T(128)S(1)}, /*index=...) while((s32[]{:T(128)}, bf16[4,1152]{1,0:T(4,128)(2,1)S(1)}, ...), condition=%wide.region_3.4_spmd.clone, body=%wide.region_2.3_spmd.clone.sunk | while | flops 484565 | bytes 406372 | solution.py:126
  130.6 5.0 collective-permute-done
  135.6 3.4 collective-permute-done.1
  143.9 5.4 collective-permute-done
  149.4 3.0 collective-permute-done.1
  157.3 5.4 collective-permute-done
  162.7 3.0 collective-permute-done.1
  170.7 5.4 collective-permute-done
  176.1 3.0 collective-permute-done.1
  184.1 5.4 collective-permute-done
  189.5 3.0 collective-permute-done.1
  197.5 5.4 collective-permute-done
  202.9 3.0 collective-permute-done.1
  210.9 5.4 collective-permute-done
  216.3 3.0 collective-permute-done.1
  224.3 5.4 collective-permute-done
  229.7 3.0 collective-permute-done.1
  237.7 5.4 collective-permute-done
  243.1 3.0 collective-permute-done.1
  251.1 5.6 collective-permute-done
  264.5 5.4 collective-permute-done
  269.9 3.0 collective-permute-done.1
  277.8 5.4 collective-permute-done
  291.2 5.4 collective-permute-done
  304.6 5.4 collective-permute-done
  318.0 5.4 collective-permute-done
  331.4 5.4 collective-permute-done
  339.8 196.7 %while.41 = (s32[]{:T(128)}, bf16[4,1152]{1,0:T(4,128)(2,1)S(1)}, f32[4,1152]{1,0:T(4,128)S(1)}, f32[16,1152]{1,0:T(8,128)S(1)}, s32[16]{0:T(128)S(1)}, /*index=...) while((s32[]{:T(128)}, bf16[4,1152]{1,0:T(4,128)(2,1)S(1)}, ...), condition=%wide.region_5.6_spmd.clone, body=%wide.region_4.5_spmd.clone.sunk | while | flops 470742 | bytes 443248 | solution.py:129
  339.8 3.4 collective-permute-start.2
  347.8 7.9 %collective-permute-start.2 = (bf16[4,1152]{1,0:T(4,128)(2,1)S(1)}, bf16[4,1152]{1,0:T(4,128)(2,1)S(1)}, u32[]{:S(2)}, u32[]{:S(2)}) collective-permute-start(bf16[4,1152]{1,0:T(4,128)(2,1)S(1)} %get-tuple-element.787), channel_id=1, source_target_pairs={{0,508},{4,0},{8,4},{12,8},{16,12},{20,16},{24,20},{28,24},{32,28}... | collective-permute-start | bytes 27656 | tf_op jit(solution)/shard_map/while/body/eval_jaxpr/ppermute | solution.py:38
  360.4 7.9 %collective-permute-start.2 = (bf16[4,1152]{1,0:T(4,128)(2,1)S(1)}, bf16[4,1152]{1,0:T(4,128)(2,1)S(1)}, u32[]{:S(2)}, u32[]{:S(2)}) collective-permute-start(bf16[4,1152]{1,0:T(4,128)(2,1)S(1)} %get-tuple-element.787), channel_id=1, source_target_pairs={{0,508},{4,0},{8,4},{12,8},{16,12},{20,16},{24,20},{28,24},{32,28}... | collective-permute-start | bytes 27656 | tf_op jit(solution)/shard_map/while/body/eval_jaxpr/ppermute | solution.py:38
  373.0 7.9 %collective-permute-start.2 = (bf16[4,1152]{1,0:T(4,128)(2,1)S(1)}, bf16[4,1152]{1,0:T(4,128)(2,1)S(1)}, u32[]{:S(2)}, u32[]{:S(2)}) collective-permute-start(bf16[4,1152]{1,0:T(4,128)(2,1)S(1)} %get-tuple-element.787), channel_id=1, source_target_pairs={{0,508},{4,0},{8,4},{12,8},{16,12},{20,16},{24,20},{28,24},{32,28}... | collective-permute-start | bytes 27656 | tf_op jit(solution)/shard_map/while/body/eval_jaxpr/ppermute | solution.py:38
  385.5 7.9 %collective-permute-start.2 = (bf16[4,1152]{1,0:T(4,128)(2,1)S(1)}, bf16[4,1152]{1,0:T(4,128)(2,1)S(1)}, u32[]{:S(2)}, u32[]{:S(2)}) collective-permute-start(bf16[4,1152]{1,0:T(4,128)(2,1)S(1)} %get-tuple-element.787), channel_id=1, source_target_pairs={{0,508},{4,0},{8,4},{12,8},{16,12},{20,16},{24,20},{28,24},{32,28}... | collective-permute-start | bytes 27656 | tf_op jit(solution)/shard_map/while/body/eval_jaxpr/ppermute | solution.py:38
  398.1 7.9 %collective-permute-start.2 = (bf16[4,1152]{1,0:T(4,128)(2,1)S(1)}, bf16[4,1152]{1,0:T(4,128)(2,1)S(1)}, u32[]{:S(2)}, u32[]{:S(2)}) collective-permute-start(bf16[4,1152]{1,0:T(4,128)(2,1)S(1)} %get-tuple-element.787), channel_id=1, source_target_pairs={{0,508},{4,0},{8,4},{12,8},{16,12},{20,16},{24,20},{28,24},{32,28}... | collective-permute-start | bytes 27656 | tf_op jit(solution)/shard_map/while/body/eval_jaxpr/ppermute | solution.py:38
  410.7 7.9 %collective-permute-start.2 = (bf16[4,1152]{1,0:T(4,128)(2,1)S(1)}, bf16[4,1152]{1,0:T(4,128)(2,1)S(1)}, u32[]{:S(2)}, u32[]{:S(2)}) collective-permute-start(bf16[4,1152]{1,0:T(4,128)(2,1)S(1)} %get-tuple-element.787), channel_id=1, source_target_pairs={{0,508},{4,0},{8,4},{12,8},{16,12},{20,16},{24,20},{28,24},{32,28}... | collective-permute-start | bytes 27656 | tf_op jit(solution)/shard_map/while/body/eval_jaxpr/ppermute | solution.py:38
  423.3 7.9 %collective-permute-start.2 = (bf16[4,1152]{1,0:T(4,128)(2,1)S(1)}, bf16[4,1152]{1,0:T(4,128)(2,1)S(1)}, u32[]{:S(2)}, u32[]{:S(2)}) collective-permute-start(bf16[4,1152]{1,0:T(4,128)(2,1)S(1)} %get-tuple-element.787), channel_id=1, source_target_pairs={{0,508},{4,0},{8,4},{12,8},{16,12},{20,16},{24,20},{28,24},{32,28}... | collective-permute-start | bytes 27656 | tf_op jit(solution)/shard_map/while/body/eval_jaxpr/ppermute | solution.py:38
  435.9 7.9 %collective-permute-start.2 = (bf16[4,1152]{1,0:T(4,128)(2,1)S(1)}, bf16[4,1152]{1,0:T(4,128)(2,1)S(1)}, u32[]{:S(2)}, u32[]{:S(2)}) collective-permute-start(bf16[4,1152]{1,0:T(4,128)(2,1)S(1)} %get-tuple-element.787), channel_id=1, source_target_pairs={{0,508},{4,0},{8,4},{12,8},{16,12},{20,16},{24,20},{28,24},{32,28}... | collective-permute-start | bytes 27656 | tf_op jit(solution)/shard_map/while/body/eval_jaxpr/ppermute | solution.py:38
  448.4 7.9 %collective-permute-start.2 = (bf16[4,1152]{1,0:T(4,128)(2,1)S(1)}, bf16[4,1152]{1,0:T(4,128)(2,1)S(1)}, u32[]{:S(2)}, u32[]{:S(2)}) collective-permute-start(bf16[4,1152]{1,0:T(4,128)(2,1)S(1)} %get-tuple-element.787), channel_id=1, source_target_pairs={{0,508},{4,0},{8,4},{12,8},{16,12},{20,16},{24,20},{28,24},{32,28}... | collective-permute-start | bytes 27656 | tf_op jit(solution)/shard_map/while/body/eval_jaxpr/ppermute | solution.py:38
  461.0 7.9 %collective-permute-start.2 = (bf16[4,1152]{1,0:T(4,128)(2,1)S(1)}, bf16[4,1152]{1,0:T(4,128)(2,1)S(1)}, u32[]{:S(2)}, u32[]{:S(2)}) collective-permute-start(bf16[4,1152]{1,0:T(4,128)(2,1)S(1)} %get-tuple-element.787), channel_id=1, source_target_pairs={{0,508},{4,0},{8,4},{12,8},{16,12},{20,16},{24,20},{28,24},{32,28}... | collective-permute-start | bytes 27656 | tf_op jit(solution)/shard_map/while/body/eval_jaxpr/ppermute | solution.py:38
  473.6 7.9 %collective-permute-start.2 = (bf16[4,1152]{1,0:T(4,128)(2,1)S(1)}, bf16[4,1152]{1,0:T(4,128)(2,1)S(1)}, u32[]{:S(2)}, u32[]{:S(2)}) collective-permute-start(bf16[4,1152]{1,0:T(4,128)(2,1)S(1)} %get-tuple-element.787), channel_id=1, source_target_pairs={{0,508},{4,0},{8,4},{12,8},{16,12},{20,16},{24,20},{28,24},{32,28}... | collective-permute-start | bytes 27656 | tf_op jit(solution)/shard_map/while/body/eval_jaxpr/ppermute | solution.py:38
  486.2 7.9 %collective-permute-start.2 = (bf16[4,1152]{1,0:T(4,128)(2,1)S(1)}, bf16[4,1152]{1,0:T(4,128)(2,1)S(1)}, u32[]{:S(2)}, u32[]{:S(2)}) collective-permute-start(bf16[4,1152]{1,0:T(4,128)(2,1)S(1)} %get-tuple-element.787), channel_id=1, source_target_pairs={{0,508},{4,0},{8,4},{12,8},{16,12},{20,16},{24,20},{28,24},{32,28}... | collective-permute-start | bytes 27656 | tf_op jit(solution)/shard_map/while/body/eval_jaxpr/ppermute | solution.py:38
  498.8 7.9 %collective-permute-start.2 = (bf16[4,1152]{1,0:T(4,128)(2,1)S(1)}, bf16[4,1152]{1,0:T(4,128)(2,1)S(1)}, u32[]{:S(2)}, u32[]{:S(2)}) collective-permute-start(bf16[4,1152]{1,0:T(4,128)(2,1)S(1)} %get-tuple-element.787), channel_id=1, source_target_pairs={{0,508},{4,0},{8,4},{12,8},{16,12},{20,16},{24,20},{28,24},{32,28}... | collective-permute-start | bytes 27656 | tf_op jit(solution)/shard_map/while/body/eval_jaxpr/ppermute | solution.py:38
  511.3 7.9 %collective-permute-start.2 = (bf16[4,1152]{1,0:T(4,128)(2,1)S(1)}, bf16[4,1152]{1,0:T(4,128)(2,1)S(1)}, u32[]{:S(2)}, u32[]{:S(2)}) collective-permute-start(bf16[4,1152]{1,0:T(4,128)(2,1)S(1)} %get-tuple-element.787), channel_id=1, source_target_pairs={{0,508},{4,0},{8,4},{12,8},{16,12},{20,16},{24,20},{28,24},{32,28}... | collective-permute-start | bytes 27656 | tf_op jit(solution)/shard_map/while/body/eval_jaxpr/ppermute | solution.py:38
  523.9 7.9 %collective-permute-start.2 = (bf16[4,1152]{1,0:T(4,128)(2,1)S(1)}, bf16[4,1152]{1,0:T(4,128)(2,1)S(1)}, u32[]{:S(2)}, u32[]{:S(2)}) collective-permute-start(bf16[4,1152]{1,0:T(4,128)(2,1)S(1)} %get-tuple-element.787), channel_id=1, source_target_pairs={{0,508},{4,0},{8,4},{12,8},{16,12},{20,16},{24,20},{28,24},{32,28}... | collective-permute-start | bytes 27656 | tf_op jit(solution)/shard_map/while/body/eval_jaxpr/ppermute | solution.py:38
  538.4 6.4 %collective-permute-start.4 = (f32[4,1152]{1,0:T(4,128)S(1)}, f32[4,1152]{1,0:T(4,128)S(1)}, u32[]{:S(2)}, u32[]{:S(2)}) collective-permute-start(f32[4,1152]{1,0:T(4,128)S(1)} %get-tuple-element.496), channel_id=1, source_target_pairs={{0,448},{4,452},{8,456},{12,460},{16,464},{20,468},{24,472},{28,47... | collective-permute-start | bytes 55304 | tf_op jit(solution)/shard_map/ppermute | solution.py:38
  545.6 42.0 %all-to-all-start.10 = ((f32[4,16,288]{2,1,0:T(8,128)}), f32[4,16,288]{2,1,0:T(8,128)S(1)}, u32[]{:S(2)}, u32[]{:S(2)}) async-start(f32[4,16,288]{2,1,0:T(8,128)} %copy.54), calls=%async_computation.10 | async-start | bytes 196608 | tf_op jit(solution)/shard_map/all_to_all | solution.py:48
  588.2 6.6 %all-to-all-done.10 = f32[4,16,288]{2,1,0:T(8,128)S(1)} async-done(((f32[4,16,288]{2,1,0:T(8,128)}), f32[4,16,288]{2,1,0:T(8,128)S(1)}, u32[]{:S(2)}, u32[]{:S(2)}) %all-to-all-start.10) | async-done | bytes 73760 | tf_op jit(solution)/shard_map/all_to_all | solution.py:48
  (317 shorter events, 189.3 us)
Async XLA Ops:
  12.5 7.8 %all-to-all-start.5 = ((bf16[4,1,12,288]{3,2,1,0:T(8,128)(2,1)}), bf16[4,1,12,288]{3,2,1,0:T(8,128)(2,1)S(1)}, u32[]{:S(2)}, u32[]{:S(2)}) async-start(bf16[4,1,12,288]{3,2,1,0:T(8,128)(2,1)} %stack.35), calls=%async_computation.5 | async-start | bytes 98304 | tf_op jit(solution)/shard_map/all_to_all | solution.py:23
  21.0 19.8 %all-to-all-start.1 = ((bf16[8,4,12,288]{3,1,2,0:T(4,128)(2,1)}), bf16[8,4,12,288]{3,1,2,0:T(4,128)(2,1)S(1)}, u32[]{:S(2)}, u32[]{:S(2)}) async-start(bf16[8,4,12,288]{3,1,2,0:T(4,128)(2,1)} %stack.31), calls=%async_computation.1 | async-start | bytes 589824 | tf_op jit(solution)/shard_map/all_to_all | solution.py:23
  41.7 13.0 %all-to-all-start.6 = ((bf16[8,4,12,288]{3,1,2,0:T(4,128)(2,1)}), bf16[8,4,12,288]{3,1,2,0:T(4,128)(2,1)S(1)}, u32[]{:S(2)}, u32[]{:S(2)}) async-start(bf16[8,4,12,288]{3,1,2,0:T(4,128)(2,1)} %stack.36), calls=%async_computation.6 | async-start | bytes 589824 | tf_op jit(solution)/shard_map/all_to_all | solution.py:23
  55.9 14.5 %all-to-all-start.2 = ((bf16[4,32,12,288]{3,1,2,0:T(8,128)(2,1)}), bf16[4,32,12,288]{3,1,2,0:T(8,128)(2,1)S(1)}, u32[]{:S(2)}, u32[]{:S(2)}) async-start(bf16[4,32,12,288]{3,1,2,0:T(8,128)(2,1)} %stack.32), calls=%async_computation.2 | async-start | bytes 2359296 | tf_op jit(solution)/shard_map/all_to_all | solution.py:23
  71.5 13.9 %all-to-all-start.7 = ((bf16[4,32,12,288]{3,1,2,0:T(8,128)(2,1)}), bf16[4,32,12,288]{3,1,2,0:T(8,128)(2,1)S(1)}, u32[]{:S(2)}, u32[]{:S(2)}) async-start(bf16[4,32,12,288]{3,1,2,0:T(8,128)(2,1)} %stack.37), calls=%async_computation.7 | async-start | bytes 2359296 | tf_op jit(solution)/shard_map/all_to_all | solution.py:23
  85.5 11.4 %all-to-all-start.3 = ((bf16[2,1,16,288]{3,2,1,0:T(8,128)(2,1)}), bf16[2,1,16,288]{3,2,1,0:T(8,128)(2,1)S(1)}, u32[]{:S(2)}, u32[]{:S(2)}) async-start(bf16[2,1,16,288]{3,2,1,0:T(8,128)(2,1)} %pad_maximum_fusion.2), calls=%async_computation.3 | async-start | bytes 49152 | tf_op jit(solution)/shard_map/all_to_all | solution.py:23
  109.9 9.9 %all-to-all-start.8 = ((bf16[2,1,16,288]{3,2,1,0:T(8,128)(2,1)}), bf16[2,1,16,288]{3,2,1,0:T(8,128)(2,1)S(1)}, u32[]{:S(2)}, u32[]{:S(2)}) async-start(bf16[2,1,16,288]{3,2,1,0:T(8,128)(2,1)} %pad_maximum_fusion.3), calls=%async_computation.8 | async-start | bytes 49152 | tf_op jit(solution)/shard_map/all_to_all | solution.py:23
  125.2 10.4 %collective-permute-start = (bf16[4,1152]{1,0:T(4,128)(2,1)S(1)}, bf16[4,1152]{1,0:T(4,128)(2,1)S(1)}, u32[]{:S(2)}, u32[]{:S(2)}) collective-permute-start(bf16[4,1152]{1,0:T(4,128)(2,1)S(1)} %copy.60), channel_id=1, source_target_pairs={{0,4},{4,8},{8,12},{12,16},{16,20},{20,24},{24,28},{28,32},{32,36}... | collective-permute-start | bytes 27656 | tf_op jit(solution)/shard_map/while/body/eval_jaxpr/ppermute | solution.py:38
  128.4 10.5 %collective-permute-start.1 = (f32[4,1152]{1,0:T(4,128)S(1)}, f32[4,1152]{1,0:T(4,128)S(1)}, u32[]{:S(2)}, u32[]{:S(2)}) collective-permute-start(f32[4,1152]{1,0:T(4,128)S(1)} %convolution_add_fusion.8), channel_id=1, source_target_pairs={{0,4},{4,8},{8,12},{12,16},{16,20},{20,24},{24,28},{28,32},{32,36}... | collective-permute-start | bytes 55304 | tf_op jit(solution)/shard_map/while/body/eval_jaxpr/ppermute | solution.py:38
  138.9 10.4 %collective-permute-start = (bf16[4,1152]{1,0:T(4,128)(2,1)S(1)}, bf16[4,1152]{1,0:T(4,128)(2,1)S(1)}, u32[]{:S(2)}, u32[]{:S(2)}) collective-permute-start(bf16[4,1152]{1,0:T(4,128)(2,1)S(1)} %copy.60), channel_id=1, source_target_pairs={{0,4},{4,8},{8,12},{12,16},{16,20},{20,24},{24,28},{28,32},{32,36}... | collective-permute-start | bytes 27656 | tf_op jit(solution)/shard_map/while/body/eval_jaxpr/ppermute | solution.py:38
  141.8 10.5 %collective-permute-start.1 = (f32[4,1152]{1,0:T(4,128)S(1)}, f32[4,1152]{1,0:T(4,128)S(1)}, u32[]{:S(2)}, u32[]{:S(2)}) collective-permute-start(f32[4,1152]{1,0:T(4,128)S(1)} %convolution_add_fusion.8), channel_id=1, source_target_pairs={{0,4},{4,8},{8,12},{12,16},{16,20},{20,24},{24,28},{28,32},{32,36}... | collective-permute-start | bytes 55304 | tf_op jit(solution)/shard_map/while/body/eval_jaxpr/ppermute | solution.py:38
  152.3 10.4 %collective-permute-start = (bf16[4,1152]{1,0:T(4,128)(2,1)S(1)}, bf16[4,1152]{1,0:T(4,128)(2,1)S(1)}, u32[]{:S(2)}, u32[]{:S(2)}) collective-permute-start(bf16[4,1152]{1,0:T(4,128)(2,1)S(1)} %copy.60), channel_id=1, source_target_pairs={{0,4},{4,8},{8,12},{12,16},{16,20},{20,24},{24,28},{28,32},{32,36}... | collective-permute-start | bytes 27656 | tf_op jit(solution)/shard_map/while/body/eval_jaxpr/ppermute | solution.py:38
  155.2 10.5 %collective-permute-start.1 = (f32[4,1152]{1,0:T(4,128)S(1)}, f32[4,1152]{1,0:T(4,128)S(1)}, u32[]{:S(2)}, u32[]{:S(2)}) collective-permute-start(f32[4,1152]{1,0:T(4,128)S(1)} %convolution_add_fusion.8), channel_id=1, source_target_pairs={{0,4},{4,8},{8,12},{12,16},{16,20},{20,24},{24,28},{28,32},{32,36}... | collective-permute-start | bytes 55304 | tf_op jit(solution)/shard_map/while/body/eval_jaxpr/ppermute | solution.py:38
  165.7 10.4 %collective-permute-start = (bf16[4,1152]{1,0:T(4,128)(2,1)S(1)}, bf16[4,1152]{1,0:T(4,128)(2,1)S(1)}, u32[]{:S(2)}, u32[]{:S(2)}) collective-permute-start(bf16[4,1152]{1,0:T(4,128)(2,1)S(1)} %copy.60), channel_id=1, source_target_pairs={{0,4},{4,8},{8,12},{12,16},{16,20},{20,24},{24,28},{28,32},{32,36}... | collective-permute-start | bytes 27656 | tf_op jit(solution)/shard_map/while/body/eval_jaxpr/ppermute | solution.py:38
  168.6 10.5 %collective-permute-start.1 = (f32[4,1152]{1,0:T(4,128)S(1)}, f32[4,1152]{1,0:T(4,128)S(1)}, u32[]{:S(2)}, u32[]{:S(2)}) collective-permute-start(f32[4,1152]{1,0:T(4,128)S(1)} %convolution_add_fusion.8), channel_id=1, source_target_pairs={{0,4},{4,8},{8,12},{12,16},{16,20},{20,24},{24,28},{28,32},{32,36}... | collective-permute-start | bytes 55304 | tf_op jit(solution)/shard_map/while/body/eval_jaxpr/ppermute | solution.py:38
  179.1 10.4 %collective-permute-start = (bf16[4,1152]{1,0:T(4,128)(2,1)S(1)}, bf16[4,1152]{1,0:T(4,128)(2,1)S(1)}, u32[]{:S(2)}, u32[]{:S(2)}) collective-permute-start(bf16[4,1152]{1,0:T(4,128)(2,1)S(1)} %copy.60), channel_id=1, source_target_pairs={{0,4},{4,8},{8,12},{12,16},{16,20},{20,24},{24,28},{28,32},{32,36}... | collective-permute-start | bytes 27656 | tf_op jit(solution)/shard_map/while/body/eval_jaxpr/ppermute | solution.py:38
  182.0 10.5 %collective-permute-start.1 = (f32[4,1152]{1,0:T(4,128)S(1)}, f32[4,1152]{1,0:T(4,128)S(1)}, u32[]{:S(2)}, u32[]{:S(2)}) collective-permute-start(f32[4,1152]{1,0:T(4,128)S(1)} %convolution_add_fusion.8), channel_id=1, source_target_pairs={{0,4},{4,8},{8,12},{12,16},{16,20},{20,24},{24,28},{28,32},{32,36}... | collective-permute-start | bytes 55304 | tf_op jit(solution)/shard_map/while/body/eval_jaxpr/ppermute | solution.py:38
  192.5 10.4 %collective-permute-start = (bf16[4,1152]{1,0:T(4,128)(2,1)S(1)}, bf16[4,1152]{1,0:T(4,128)(2,1)S(1)}, u32[]{:S(2)}, u32[]{:S(2)}) collective-permute-start(bf16[4,1152]{1,0:T(4,128)(2,1)S(1)} %copy.60), channel_id=1, source_target_pairs={{0,4},{4,8},{8,12},{12,16},{16,20},{20,24},{24,28},{28,32},{32,36}... | collective-permute-start | bytes 27656 | tf_op jit(solution)/shard_map/while/body/eval_jaxpr/ppermute | solution.py:38
  195.4 10.5 %collective-permute-start.1 = (f32[4,1152]{1,0:T(4,128)S(1)}, f32[4,1152]{1,0:T(4,128)S(1)}, u32[]{:S(2)}, u32[]{:S(2)}) collective-permute-start(f32[4,1152]{1,0:T(4,128)S(1)} %convolution_add_fusion.8), channel_id=1, source_target_pairs={{0,4},{4,8},{8,12},{12,16},{16,20},{20,24},{24,28},{28,32},{32,36}... | collective-permute-start | bytes 55304 | tf_op jit(solution)/shard_map/while/body/eval_jaxpr/ppermute | solution.py:38
  205.9 10.4 %collective-permute-start = (bf16[4,1152]{1,0:T(4,128)(2,1)S(1)}, bf16[4,1152]{1,0:T(4,128)(2,1)S(1)}, u32[]{:S(2)}, u32[]{:S(2)}) collective-permute-start(bf16[4,1152]{1,0:T(4,128)(2,1)S(1)} %copy.60), channel_id=1, source_target_pairs={{0,4},{4,8},{8,12},{12,16},{16,20},{20,24},{24,28},{28,32},{32,36}... | collective-permute-start | bytes 27656 | tf_op jit(solution)/shard_map/while/body/eval_jaxpr/ppermute | solution.py:38
  208.8 10.5 %collective-permute-start.1 = (f32[4,1152]{1,0:T(4,128)S(1)}, f32[4,1152]{1,0:T(4,128)S(1)}, u32[]{:S(2)}, u32[]{:S(2)}) collective-permute-start(f32[4,1152]{1,0:T(4,128)S(1)} %convolution_add_fusion.8), channel_id=1, source_target_pairs={{0,4},{4,8},{8,12},{12,16},{16,20},{20,24},{24,28},{28,32},{32,36}... | collective-permute-start | bytes 55304 | tf_op jit(solution)/shard_map/while/body/eval_jaxpr/ppermute | solution.py:38
  219.3 10.4 %collective-permute-start = (bf16[4,1152]{1,0:T(4,128)(2,1)S(1)}, bf16[4,1152]{1,0:T(4,128)(2,1)S(1)}, u32[]{:S(2)}, u32[]{:S(2)}) collective-permute-start(bf16[4,1152]{1,0:T(4,128)(2,1)S(1)} %copy.60), channel_id=1, source_target_pairs={{0,4},{4,8},{8,12},{12,16},{16,20},{20,24},{24,28},{28,32},{32,36}... | collective-permute-start | bytes 27656 | tf_op jit(solution)/shard_map/while/body/eval_jaxpr/ppermute | solution.py:38
  222.1 10.5 %collective-permute-start.1 = (f32[4,1152]{1,0:T(4,128)S(1)}, f32[4,1152]{1,0:T(4,128)S(1)}, u32[]{:S(2)}, u32[]{:S(2)}) collective-permute-start(f32[4,1152]{1,0:T(4,128)S(1)} %convolution_add_fusion.8), channel_id=1, source_target_pairs={{0,4},{4,8},{8,12},{12,16},{16,20},{20,24},{24,28},{28,32},{32,36}... | collective-permute-start | bytes 55304 | tf_op jit(solution)/shard_map/while/body/eval_jaxpr/ppermute | solution.py:38
  232.7 10.4 %collective-permute-start = (bf16[4,1152]{1,0:T(4,128)(2,1)S(1)}, bf16[4,1152]{1,0:T(4,128)(2,1)S(1)}, u32[]{:S(2)}, u32[]{:S(2)}) collective-permute-start(bf16[4,1152]{1,0:T(4,128)(2,1)S(1)} %copy.60), channel_id=1, source_target_pairs={{0,4},{4,8},{8,12},{12,16},{16,20},{20,24},{24,28},{28,32},{32,36}... | collective-permute-start | bytes 27656 | tf_op jit(solution)/shard_map/while/body/eval_jaxpr/ppermute | solution.py:38
  235.5 10.5 %collective-permute-start.1 = (f32[4,1152]{1,0:T(4,128)S(1)}, f32[4,1152]{1,0:T(4,128)S(1)}, u32[]{:S(2)}, u32[]{:S(2)}) collective-permute-start(f32[4,1152]{1,0:T(4,128)S(1)} %convolution_add_fusion.8), channel_id=1, source_target_pairs={{0,4},{4,8},{8,12},{12,16},{16,20},{20,24},{24,28},{28,32},{32,36}... | collective-permute-start | bytes 55304 | tf_op jit(solution)/shard_map/while/body/eval_jaxpr/ppermute | solution.py:38
  246.1 10.6 %collective-permute-start = (bf16[4,1152]{1,0:T(4,128)(2,1)S(1)}, bf16[4,1152]{1,0:T(4,128)(2,1)S(1)}, u32[]{:S(2)}, u32[]{:S(2)}) collective-permute-start(bf16[4,1152]{1,0:T(4,128)(2,1)S(1)} %copy.60), channel_id=1, source_target_pairs={{0,4},{4,8},{8,12},{12,16},{16,20},{20,24},{24,28},{28,32},{32,36}... | collective-permute-start | bytes 27656 | tf_op jit(solution)/shard_map/while/body/eval_jaxpr/ppermute | solution.py:38
  248.9 10.5 %collective-permute-start.1 = (f32[4,1152]{1,0:T(4,128)S(1)}, f32[4,1152]{1,0:T(4,128)S(1)}, u32[]{:S(2)}, u32[]{:S(2)}) collective-permute-start(f32[4,1152]{1,0:T(4,128)S(1)} %convolution_add_fusion.8), channel_id=1, source_target_pairs={{0,4},{4,8},{8,12},{12,16},{16,20},{20,24},{24,28},{28,32},{32,36}... | collective-permute-start | bytes 55304 | tf_op jit(solution)/shard_map/while/body/eval_jaxpr/ppermute | solution.py:38
  259.4 10.4 %collective-permute-start = (bf16[4,1152]{1,0:T(4,128)(2,1)S(1)}, bf16[4,1152]{1,0:T(4,128)(2,1)S(1)}, u32[]{:S(2)}, u32[]{:S(2)}) collective-permute-start(bf16[4,1152]{1,0:T(4,128)(2,1)S(1)} %copy.60), channel_id=1, source_target_pairs={{0,4},{4,8},{8,12},{12,16},{16,20},{20,24},{24,28},{28,32},{32,36}... | collective-permute-start | bytes 27656 | tf_op jit(solution)/shard_map/while/body/eval_jaxpr/ppermute | solution.py:38
  262.3 10.5 %collective-permute-start.1 = (f32[4,1152]{1,0:T(4,128)S(1)}, f32[4,1152]{1,0:T(4,128)S(1)}, u32[]{:S(2)}, u32[]{:S(2)}) collective-permute-start(f32[4,1152]{1,0:T(4,128)S(1)} %convolution_add_fusion.8), channel_id=1, source_target_pairs={{0,4},{4,8},{8,12},{12,16},{16,20},{20,24},{24,28},{28,32},{32,36}... | collective-permute-start | bytes 55304 | tf_op jit(solution)/shard_map/while/body/eval_jaxpr/ppermute | solution.py:38
  272.8 10.4 %collective-permute-start = (bf16[4,1152]{1,0:T(4,128)(2,1)S(1)}, bf16[4,1152]{1,0:T(4,128)(2,1)S(1)}, u32[]{:S(2)}, u32[]{:S(2)}) collective-permute-start(bf16[4,1152]{1,0:T(4,128)(2,1)S(1)} %copy.60), channel_id=1, source_target_pairs={{0,4},{4,8},{8,12},{12,16},{16,20},{20,24},{24,28},{28,32},{32,36}... | collective-permute-start | bytes 27656 | tf_op jit(solution)/shard_map/while/body/eval_jaxpr/ppermute | solution.py:38
  275.7 10.5 %collective-permute-start.1 = (f32[4,1152]{1,0:T(4,128)S(1)}, f32[4,1152]{1,0:T(4,128)S(1)}, u32[]{:S(2)}, u32[]{:S(2)}) collective-permute-start(f32[4,1152]{1,0:T(4,128)S(1)} %convolution_add_fusion.8), channel_id=1, source_target_pairs={{0,4},{4,8},{8,12},{12,16},{16,20},{20,24},{24,28},{28,32},{32,36}... | collective-permute-start | bytes 55304 | tf_op jit(solution)/shard_map/while/body/eval_jaxpr/ppermute | solution.py:38
  286.2 10.4 %collective-permute-start = (bf16[4,1152]{1,0:T(4,128)(2,1)S(1)}, bf16[4,1152]{1,0:T(4,128)(2,1)S(1)}, u32[]{:S(2)}, u32[]{:S(2)}) collective-permute-start(bf16[4,1152]{1,0:T(4,128)(2,1)S(1)} %copy.60), channel_id=1, source_target_pairs={{0,4},{4,8},{8,12},{12,16},{16,20},{20,24},{24,28},{28,32},{32,36}... | collective-permute-start | bytes 27656 | tf_op jit(solution)/shard_map/while/body/eval_jaxpr/ppermute | solution.py:38
  289.1 10.5 %collective-permute-start.1 = (f32[4,1152]{1,0:T(4,128)S(1)}, f32[4,1152]{1,0:T(4,128)S(1)}, u32[]{:S(2)}, u32[]{:S(2)}) collective-permute-start(f32[4,1152]{1,0:T(4,128)S(1)} %convolution_add_fusion.8), channel_id=1, source_target_pairs={{0,4},{4,8},{8,12},{12,16},{16,20},{20,24},{24,28},{28,32},{32,36}... | collective-permute-start | bytes 55304 | tf_op jit(solution)/shard_map/while/body/eval_jaxpr/ppermute | solution.py:38
  299.6 10.4 %collective-permute-start = (bf16[4,1152]{1,0:T(4,128)(2,1)S(1)}, bf16[4,1152]{1,0:T(4,128)(2,1)S(1)}, u32[]{:S(2)}, u32[]{:S(2)}) collective-permute-start(bf16[4,1152]{1,0:T(4,128)(2,1)S(1)} %copy.60), channel_id=1, source_target_pairs={{0,4},{4,8},{8,12},{12,16},{16,20},{20,24},{24,28},{28,32},{32,36}... | collective-permute-start | bytes 27656 | tf_op jit(solution)/shard_map/while/body/eval_jaxpr/ppermute | solution.py:38
  302.5 10.5 %collective-permute-start.1 = (f32[4,1152]{1,0:T(4,128)S(1)}, f32[4,1152]{1,0:T(4,128)S(1)}, u32[]{:S(2)}, u32[]{:S(2)}) collective-permute-start(f32[4,1152]{1,0:T(4,128)S(1)} %convolution_add_fusion.8), channel_id=1, source_target_pairs={{0,4},{4,8},{8,12},{12,16},{16,20},{20,24},{24,28},{28,32},{32,36}... | collective-permute-start | bytes 55304 | tf_op jit(solution)/shard_map/while/body/eval_jaxpr/ppermute | solution.py:38
  313.0 10.4 %collective-permute-start = (bf16[4,1152]{1,0:T(4,128)(2,1)S(1)}, bf16[4,1152]{1,0:T(4,128)(2,1)S(1)}, u32[]{:S(2)}, u32[]{:S(2)}) collective-permute-start(bf16[4,1152]{1,0:T(4,128)(2,1)S(1)} %copy.60), channel_id=1, source_target_pairs={{0,4},{4,8},{8,12},{12,16},{16,20},{20,24},{24,28},{28,32},{32,36}... | collective-permute-start | bytes 27656 | tf_op jit(solution)/shard_map/while/body/eval_jaxpr/ppermute | solution.py:38
  315.9 10.5 %collective-permute-start.1 = (f32[4,1152]{1,0:T(4,128)S(1)}, f32[4,1152]{1,0:T(4,128)S(1)}, u32[]{:S(2)}, u32[]{:S(2)}) collective-permute-start(f32[4,1152]{1,0:T(4,128)S(1)} %convolution_add_fusion.8), channel_id=1, source_target_pairs={{0,4},{4,8},{8,12},{12,16},{16,20},{20,24},{24,28},{28,32},{32,36}... | collective-permute-start | bytes 55304 | tf_op jit(solution)/shard_map/while/body/eval_jaxpr/ppermute | solution.py:38
  326.4 10.4 %collective-permute-start = (bf16[4,1152]{1,0:T(4,128)(2,1)S(1)}, bf16[4,1152]{1,0:T(4,128)(2,1)S(1)}, u32[]{:S(2)}, u32[]{:S(2)}) collective-permute-start(bf16[4,1152]{1,0:T(4,128)(2,1)S(1)} %copy.60), channel_id=1, source_target_pairs={{0,4},{4,8},{8,12},{12,16},{16,20},{20,24},{24,28},{28,32},{32,36}... | collective-permute-start | bytes 27656 | tf_op jit(solution)/shard_map/while/body/eval_jaxpr/ppermute | solution.py:38
  329.3 10.5 %collective-permute-start.1 = (f32[4,1152]{1,0:T(4,128)S(1)}, f32[4,1152]{1,0:T(4,128)S(1)}, u32[]{:S(2)}, u32[]{:S(2)}) collective-permute-start(f32[4,1152]{1,0:T(4,128)S(1)} %convolution_add_fusion.8), channel_id=1, source_target_pairs={{0,4},{4,8},{8,12},{12,16},{16,20},{20,24},{24,28},{28,32},{32,36}... | collective-permute-start | bytes 55304 | tf_op jit(solution)/shard_map/while/body/eval_jaxpr/ppermute | solution.py:38
  339.8 5.3 collective-permute-start.2
  343.2 4.5 collective-permute-start.3
  347.8 9.9 %collective-permute-start.2 = (bf16[4,1152]{1,0:T(4,128)(2,1)S(1)}, bf16[4,1152]{1,0:T(4,128)(2,1)S(1)}, u32[]{:S(2)}, u32[]{:S(2)}) collective-permute-start(bf16[4,1152]{1,0:T(4,128)(2,1)S(1)} %get-tuple-element.787), channel_id=1, source_target_pairs={{0,508},{4,0},{8,4},{12,8},{16,12},{20,16},{24,20},{28,24},{32,28}... | collective-permute-start | bytes 27656 | tf_op jit(solution)/shard_map/while/body/eval_jaxpr/ppermute | solution.py:38
  355.7 4.5 collective-permute-start.3
  360.4 9.9 %collective-permute-start.2 = (bf16[4,1152]{1,0:T(4,128)(2,1)S(1)}, bf16[4,1152]{1,0:T(4,128)(2,1)S(1)}, u32[]{:S(2)}, u32[]{:S(2)}) collective-permute-start(bf16[4,1152]{1,0:T(4,128)(2,1)S(1)} %get-tuple-element.787), channel_id=1, source_target_pairs={{0,508},{4,0},{8,4},{12,8},{16,12},{20,16},{24,20},{28,24},{32,28}... | collective-permute-start | bytes 27656 | tf_op jit(solution)/shard_map/while/body/eval_jaxpr/ppermute | solution.py:38
  368.3 4.5 collective-permute-start.3
  373.0 9.9 %collective-permute-start.2 = (bf16[4,1152]{1,0:T(4,128)(2,1)S(1)}, bf16[4,1152]{1,0:T(4,128)(2,1)S(1)}, u32[]{:S(2)}, u32[]{:S(2)}) collective-permute-start(bf16[4,1152]{1,0:T(4,128)(2,1)S(1)} %get-tuple-element.787), channel_id=1, source_target_pairs={{0,508},{4,0},{8,4},{12,8},{16,12},{20,16},{24,20},{28,24},{32,28}... | collective-permute-start | bytes 27656 | tf_op jit(solution)/shard_map/while/body/eval_jaxpr/ppermute | solution.py:38
  380.9 4.5 collective-permute-start.3
  385.5 9.9 %collective-permute-start.2 = (bf16[4,1152]{1,0:T(4,128)(2,1)S(1)}, bf16[4,1152]{1,0:T(4,128)(2,1)S(1)}, u32[]{:S(2)}, u32[]{:S(2)}) collective-permute-start(bf16[4,1152]{1,0:T(4,128)(2,1)S(1)} %get-tuple-element.787), channel_id=1, source_target_pairs={{0,508},{4,0},{8,4},{12,8},{16,12},{20,16},{24,20},{28,24},{32,28}... | collective-permute-start | bytes 27656 | tf_op jit(solution)/shard_map/while/body/eval_jaxpr/ppermute | solution.py:38
  393.5 4.5 collective-permute-start.3
  398.1 9.9 %collective-permute-start.2 = (bf16[4,1152]{1,0:T(4,128)(2,1)S(1)}, bf16[4,1152]{1,0:T(4,128)(2,1)S(1)}, u32[]{:S(2)}, u32[]{:S(2)}) collective-permute-start(bf16[4,1152]{1,0:T(4,128)(2,1)S(1)} %get-tuple-element.787), channel_id=1, source_target_pairs={{0,508},{4,0},{8,4},{12,8},{16,12},{20,16},{24,20},{28,24},{32,28}... | collective-permute-start | bytes 27656 | tf_op jit(solution)/shard_map/while/body/eval_jaxpr/ppermute | solution.py:38
  406.1 4.5 collective-permute-start.3
  410.7 9.9 %collective-permute-start.2 = (bf16[4,1152]{1,0:T(4,128)(2,1)S(1)}, bf16[4,1152]{1,0:T(4,128)(2,1)S(1)}, u32[]{:S(2)}, u32[]{:S(2)}) collective-permute-start(bf16[4,1152]{1,0:T(4,128)(2,1)S(1)} %get-tuple-element.787), channel_id=1, source_target_pairs={{0,508},{4,0},{8,4},{12,8},{16,12},{20,16},{24,20},{28,24},{32,28}... | collective-permute-start | bytes 27656 | tf_op jit(solution)/shard_map/while/body/eval_jaxpr/ppermute | solution.py:38
  423.3 9.9 %collective-permute-start.2 = (bf16[4,1152]{1,0:T(4,128)(2,1)S(1)}, bf16[4,1152]{1,0:T(4,128)(2,1)S(1)}, u32[]{:S(2)}, u32[]{:S(2)}) collective-permute-start(bf16[4,1152]{1,0:T(4,128)(2,1)S(1)} %get-tuple-element.787), channel_id=1, source_target_pairs={{0,508},{4,0},{8,4},{12,8},{16,12},{20,16},{24,20},{28,24},{32,28}... | collective-permute-start | bytes 27656 | tf_op jit(solution)/shard_map/while/body/eval_jaxpr/ppermute | solution.py:38
  435.9 9.9 %collective-permute-start.2 = (bf16[4,1152]{1,0:T(4,128)(2,1)S(1)}, bf16[4,1152]{1,0:T(4,128)(2,1)S(1)}, u32[]{:S(2)}, u32[]{:S(2)}) collective-permute-start(bf16[4,1152]{1,0:T(4,128)(2,1)S(1)} %get-tuple-element.787), channel_id=1, source_target_pairs={{0,508},{4,0},{8,4},{12,8},{16,12},{20,16},{24,20},{28,24},{32,28}... | collective-permute-start | bytes 27656 | tf_op jit(solution)/shard_map/while/body/eval_jaxpr/ppermute | solution.py:38
  448.4 9.9 %collective-permute-start.2 = (bf16[4,1152]{1,0:T(4,128)(2,1)S(1)}, bf16[4,1152]{1,0:T(4,128)(2,1)S(1)}, u32[]{:S(2)}, u32[]{:S(2)}) collective-permute-start(bf16[4,1152]{1,0:T(4,128)(2,1)S(1)} %get-tuple-element.787), channel_id=1, source_target_pairs={{0,508},{4,0},{8,4},{12,8},{16,12},{20,16},{24,20},{28,24},{32,28}... | collective-permute-start | bytes 27656 | tf_op jit(solution)/shard_map/while/body/eval_jaxpr/ppermute | solution.py:38
  461.0 9.9 %collective-permute-start.2 = (bf16[4,1152]{1,0:T(4,128)(2,1)S(1)}, bf16[4,1152]{1,0:T(4,128)(2,1)S(1)}, u32[]{:S(2)}, u32[]{:S(2)}) collective-permute-start(bf16[4,1152]{1,0:T(4,128)(2,1)S(1)} %get-tuple-element.787), channel_id=1, source_target_pairs={{0,508},{4,0},{8,4},{12,8},{16,12},{20,16},{24,20},{28,24},{32,28}... | collective-permute-start | bytes 27656 | tf_op jit(solution)/shard_map/while/body/eval_jaxpr/ppermute | solution.py:38
  473.6 9.9 %collective-permute-start.2 = (bf16[4,1152]{1,0:T(4,128)(2,1)S(1)}, bf16[4,1152]{1,0:T(4,128)(2,1)S(1)}, u32[]{:S(2)}, u32[]{:S(2)}) collective-permute-start(bf16[4,1152]{1,0:T(4,128)(2,1)S(1)} %get-tuple-element.787), channel_id=1, source_target_pairs={{0,508},{4,0},{8,4},{12,8},{16,12},{20,16},{24,20},{28,24},{32,28}... | collective-permute-start | bytes 27656 | tf_op jit(solution)/shard_map/while/body/eval_jaxpr/ppermute | solution.py:38
  486.2 9.9 %collective-permute-start.2 = (bf16[4,1152]{1,0:T(4,128)(2,1)S(1)}, bf16[4,1152]{1,0:T(4,128)(2,1)S(1)}, u32[]{:S(2)}, u32[]{:S(2)}) collective-permute-start(bf16[4,1152]{1,0:T(4,128)(2,1)S(1)} %get-tuple-element.787), channel_id=1, source_target_pairs={{0,508},{4,0},{8,4},{12,8},{16,12},{20,16},{24,20},{28,24},{32,28}... | collective-permute-start | bytes 27656 | tf_op jit(solution)/shard_map/while/body/eval_jaxpr/ppermute | solution.py:38
  498.8 9.9 %collective-permute-start.2 = (bf16[4,1152]{1,0:T(4,128)(2,1)S(1)}, bf16[4,1152]{1,0:T(4,128)(2,1)S(1)}, u32[]{:S(2)}, u32[]{:S(2)}) collective-permute-start(bf16[4,1152]{1,0:T(4,128)(2,1)S(1)} %get-tuple-element.787), channel_id=1, source_target_pairs={{0,508},{4,0},{8,4},{12,8},{16,12},{20,16},{24,20},{28,24},{32,28}... | collective-permute-start | bytes 27656 | tf_op jit(solution)/shard_map/while/body/eval_jaxpr/ppermute | solution.py:38
  511.3 9.9 %collective-permute-start.2 = (bf16[4,1152]{1,0:T(4,128)(2,1)S(1)}, bf16[4,1152]{1,0:T(4,128)(2,1)S(1)}, u32[]{:S(2)}, u32[]{:S(2)}) collective-permute-start(bf16[4,1152]{1,0:T(4,128)(2,1)S(1)} %get-tuple-element.787), channel_id=1, source_target_pairs={{0,508},{4,0},{8,4},{12,8},{16,12},{20,16},{24,20},{28,24},{32,28}... | collective-permute-start | bytes 27656 | tf_op jit(solution)/shard_map/while/body/eval_jaxpr/ppermute | solution.py:38
  523.9 9.9 %collective-permute-start.2 = (bf16[4,1152]{1,0:T(4,128)(2,1)S(1)}, bf16[4,1152]{1,0:T(4,128)(2,1)S(1)}, u32[]{:S(2)}, u32[]{:S(2)}) collective-permute-start(bf16[4,1152]{1,0:T(4,128)(2,1)S(1)} %get-tuple-element.787), channel_id=1, source_target_pairs={{0,508},{4,0},{8,4},{12,8},{16,12},{20,16},{24,20},{28,24},{32,28}... | collective-permute-start | bytes 27656 | tf_op jit(solution)/shard_map/while/body/eval_jaxpr/ppermute | solution.py:38
  536.5 51.1 %collective-permute-start.5 = (f32[4,1152]{1,0:T(4,128)S(1)}, f32[4,1152]{1,0:T(4,128)S(1)}, u32[]{:S(2)}, u32[]{:S(2)}) collective-permute-start(f32[4,1152]{1,0:T(4,128)S(1)} %get-tuple-element.497), channel_id=1, source_target_pairs={{0,64},{4,68},{8,72},{12,76},{16,80},{20,84},{24,88},{28,92},{32,9... | collective-permute-start | bytes 55304 | tf_op jit(solution)/shard_map/ppermute | solution.py:38
  538.4 49.2 %collective-permute-start.4 = (f32[4,1152]{1,0:T(4,128)S(1)}, f32[4,1152]{1,0:T(4,128)S(1)}, u32[]{:S(2)}, u32[]{:S(2)}) collective-permute-start(f32[4,1152]{1,0:T(4,128)S(1)} %get-tuple-element.496), channel_id=1, source_target_pairs={{0,448},{4,452},{8,456},{12,460},{16,464},{20,468},{24,472},{28,47... | collective-permute-start | bytes 55304 | tf_op jit(solution)/shard_map/ppermute | solution.py:38
  545.6 49.3 %all-to-all-start.10 = ((f32[4,16,288]{2,1,0:T(8,128)}), f32[4,16,288]{2,1,0:T(8,128)S(1)}, u32[]{:S(2)}, u32[]{:S(2)}) async-start(f32[4,16,288]{2,1,0:T(8,128)} %copy.54), calls=%async_computation.10 | async-start | bytes 196608 | tf_op jit(solution)/shard_map/all_to_all | solution.py:48
  (13 other events, 156.5 us)
